TPU v7x, 32 devices: a whole 2x2x4 slice. The times are simulated.
32 devices in a mesh: fsdp: 4 (over z), tp: 8 (over y, x, core).
Axes of the slice: x: 2, y: 2, z: 4, core: 2. Of those that a mesh axis runs over, the one named last changes fastest.
Arguments:
- tokens: bfloat16 [3008, 4096], P('fsdp', 'tp'), may hold values from -6 to 6
- norm_gain: float32 [4096], replicated, may hold values from 0.5 to 1.5
- base_gate: bfloat16 [4096, 12288], P(None, 'tp'), may hold values from -0.09375 to 0.09375
- base_up: bfloat16 [4096, 12288], P(None, 'tp'), may hold values from -0.09375 to 0.09375
- base_down: bfloat16 [12288, 4096], P('tp'), may hold values from -0.0546875 to 0.0546875
- code_gate: bfloat16 [4096, 12288], P(('fsdp', 'tp')), may hold values from -4 to 4
- code_up: bfloat16 [4096, 12288], P(('fsdp', 'tp')), may hold values from -4 to 4
- scale_gate: float32 [4096, 96], P(('fsdp', 'tp')), may hold values from 0.005 to 0.05
- scale_up: float32 [4096, 96], P(('fsdp', 'tp')), may hold values from 0.005 to 0.05
- code_down: bfloat16 [12288, 4096], P(None, ('fsdp', 'tp')), may hold values from -4 to 4
- scale_down: float32 [96, 4096], P(None, ('fsdp', 'tp')), may hold values from 0.005 to 0.05
- cu_seqlens: int32 [4, 9], P('fsdp'), may hold values from 0 to 752, as said below
Outputs:
- mixed: bfloat16 [3008, 4096], P('fsdp', 'tp')
- seq_means: float32 [32, 4096], P('fsdp', 'tp')
Inputs may be any that keep to these rules, and one draw needn't show every extreme that they name: `cu_seqlens`: each row starts at 0 and rises strictly; its last entry is the group's live tokens, which fill the first slots of its 752. Over all groups the live tokens add up to exactly 1536, and some group has exactly 752.
All inputs are finite; a program needn't handle non-finite values.
Results may differ from a plain program's by a relative error of at most 0.023.
Values may be sent and summed in bfloat16 or wider, within the bound.
A program may use at most 256 MiB of HBM per device.

v0:
```python
import jax
import jax.numpy as jnp
from jax import lax
from jax.sharding import PartitionSpec as P

SEQS = 8
EPSILON = 1e-06
F32, BF16 = jnp.float32, jnp.bfloat16


def dequant_rows(base_part, code_part, scales):
    rows, cols = code_part.shape
    blocks = scales.shape[1]
    delta = code_part.astype(F32).reshape(rows, blocks, cols // blocks) * scales[:, :, None]
    return (base_part.astype(F32) + delta.reshape(rows, cols)).astype(BF16)


def dequant_cols(base_part, code_part, scales):
    rows, cols = code_part.shape
    blocks = scales.shape[0]
    delta = code_part.astype(F32).reshape(blocks, rows // blocks, cols) * scales[:, None, :]
    return (base_part.astype(F32) + delta.reshape(rows, cols)).astype(BF16)


def swap_up(part, axis_name="tp"):
    return lax.all_to_all(part, axis_name, split_axis=1, concat_axis=0, tiled=True)


def swap_down(part):
    return lax.all_to_all(part, "tp", split_axis=0, concat_axis=1, tiled=True)


def shards(tokens, norm_gain, base_gate, base_up, base_down, code_gate, code_up,
           scale_gate, scale_up, code_down, scale_down, cu_seqlens):
    groups = lax.axis_size("fsdp")
    slices = lax.axis_size("tp")
    me_f = lax.axis_index("fsdp")
    me_t = lax.axis_index("tp")
    cap, feat = tokens.shape
    width = base_gate.shape[0]
    depth = width // groups
    units = base_gate.shape[1]
    live_all = groups * (cap // 2 + SEQS)
    grain = 16 * slices
    capp = -(-cap // grain) * grain
    part = capp // slices

    padded = jnp.pad(tokens, ((0, capp - cap), (0, 0)))
    rows_full = lax.all_to_all(padded, "tp", split_axis=0, concat_axis=1, tiled=True)
    wide = rows_full.astype(F32)
    inverse = lax.rsqrt(jnp.mean(wide * wide, axis=1, keepdims=True) + EPSILON)
    normed = (wide * inverse * norm_gain[None, :]).astype(BF16)
    block = swap_up(normed, "fsdp")
    every = lax.all_gather(block, "tp", axis=0, tiled=True)

    bounds_all = lax.all_gather(cu_seqlens, "fsdp", axis=0, tiled=True)
    counts = bounds_all[:, SEQS]
    ends = jnp.cumsum(counts)
    starts = ends - counts
    place = jnp.arange(live_all, dtype=jnp.int32)
    group_of = jnp.sum((place[:, None] >= ends[None, :]).astype(jnp.int32), axis=1)
    group_of = jnp.minimum(group_of, groups - 1)
    slot = place - jnp.take(starts, group_of)
    source = (slot // part) * (groups * part) + group_of * part + slot % part
    pick = (source[:, None] == jnp.arange(slices * groups * part, dtype=jnp.int32)[None, :]).astype(BF16)
    packed = jnp.dot(pick, every, preferred_element_type=F32).astype(BF16)

    gate_rows = lax.dynamic_slice_in_dim(base_gate, me_f * depth, depth, 0)
    up_rows = lax.dynamic_slice_in_dim(base_up, me_f * depth, depth, 0)
    w_gate = dequant_rows(gate_rows, swap_up(code_gate), swap_up(scale_gate))
    w_up = dequant_rows(up_rows, swap_up(code_up), swap_up(scale_up))
    gate_part = jnp.dot(packed, w_gate, preferred_element_type=F32).astype(BF16)
    up_part = jnp.dot(packed, w_up, preferred_element_type=F32).astype(BF16)
    up_part, code_down = lax.optimization_barrier((up_part, code_down))
    gate_sum = lax.psum_scatter(gate_part, "fsdp", scatter_dimension=0, tiled=True)
    up_sum = lax.psum_scatter(up_part, "fsdp", scatter_dimension=0, tiled=True)
    down_codes, down_scales = swap_down(code_down), swap_down(scale_down)
    gate_sum, up_sum, down_codes, down_scales = lax.optimization_barrier(
        (gate_sum, up_sum, down_codes, down_scales))
    hidden = (jax.nn.silu(gate_sum.astype(F32)) * up_sum.astype(F32)).astype(BF16)
    hidden_all = lax.all_gather(hidden, "fsdp", axis=0, tiled=True)

    down_cols = lax.dynamic_slice_in_dim(base_down, me_f * depth, depth, 1)
    w_down = dequant_cols(down_cols, down_codes, down_scales)
    out_part = jnp.dot(hidden_all, w_down, preferred_element_type=F32).astype(BF16)
    out_cols = lax.psum_scatter(out_part, "tp", scatter_dimension=1, tiled=True)
    narrow = out_cols.shape[1]

    grp = jnp.arange(groups, dtype=jnp.int32)
    slots = jnp.arange(cap, dtype=jnp.int32)
    wanted = jnp.where(slots[None, :] < counts[:, None], starts[:, None] + slots[None, :], -1)
    spread = (wanted.reshape(-1)[:, None] == place[None, :]).astype(BF16)
    placed_rows = jnp.dot(spread, out_cols, preferred_element_type=F32).astype(BF16)
    mine = lax.all_to_all(placed_rows.reshape(groups, cap, narrow), "fsdp", split_axis=0, concat_axis=0, tiled=True)
    ratio = slices // groups
    span = slices // ratio
    half = me_t // span
    pick_half = (jnp.arange(ratio) == half)[None, :, None, None]
    outgoing = jnp.where(pick_half, mine[:, None], jnp.zeros((), BF16)).reshape(slices, cap, narrow)
    incoming = lax.all_to_all(outgoing, "tp", split_axis=0, concat_axis=0, tiled=True)
    take_from = lax.dynamic_slice_in_dim(incoming, (me_t % ratio) * span, span, 0)
    summed_out = take_from.transpose(1, 0, 2).reshape(cap, feat).astype(F32)

    bounds = cu_seqlens[0]
    live_count = bounds[SEQS]
    mixed = (tokens.astype(F32) + summed_out).astype(BF16)
    mixed = jnp.where((slots < live_count)[:, None], mixed, jnp.zeros((), BF16))
    member = (slots[None, :] >= bounds[:-1, None]) & (slots[None, :] < bounds[1:, None])
    seq_sums = jnp.dot(member.astype(BF16), mixed, preferred_element_type=F32)
    lengths = (bounds[1:] - bounds[:-1]).astype(F32)
    return mixed, seq_sums / lengths[:, None]


def solution(mesh):
    placed = (
        P("fsdp", "tp"), P(), P(None, "tp"), P(None, "tp"), P("tp", None),
        P(("fsdp", "tp"), None), P(("fsdp", "tp"), None),
        P(("fsdp", "tp"), None), P(("fsdp", "tp"), None),
        P(None, ("fsdp", "tp")), P(None, ("fsdp", "tp")), P("fsdp", None),
    )
    return jax.shard_map(shards, mesh=mesh, in_specs=placed,
                         out_specs=(P("fsdp", "tp"), P("fsdp", "tp")), check_vma=False)
```

profile of v0, /device:TPU:0, one launch (start us, length us, event | category | flops | bytes accessed | tf_op | source)
XLA Modules:
  0.0 536.5 jit_solution(2134350978414402686)
XLA Ops:
  7.2 2.1 pad.4
  9.3 5.2 all-to-all-start
  14.5 0.7 mul.101
  15.2 11.8 %all-to-all-done = bf16[8,96,512]{2,1,0:T(8,128)(2,1)S(1)} async-done(((bf16[8,96,512]{2,1,0:T(8,128)(2,1)}), bf16[8,96,512]{2,1,0:T(8,128)(2,1)S(1)}, u32[]{:S(2)}, u32[]{:S(2)}) %all-to-all-start) | async-done | bytes 786464 | tf_op jit(solution)/shard_map/all_to_all | solution.py:49
  27.0 0.2 convert_bitcast_fusion.2
  27.2 0.9 copy.57
  28.1 1.9 reshape.196
  30.1 0.3 fusion.17
  30.4 2.0 multiply_convert_fusion
  32.4 0.2 copy.58
  32.6 22.1 %all_to_all.135 = bf16[96,4,1024]{2,0,1:T(8,128)(2,1)} all-to-all(bf16[96,4,1024]{2,0,1:T(8,128)(2,1)S(1)} %copy.58), channel_id=1, replica_groups=mesh['fsdp'=4,'tp'=8] {'fsdp'}, dimensions={1} | all-to-all | bytes 1572864 | tf_op jit(solution)/shard_map/all_to_all | solution.py:26
  54.8 0.6 all_to_all.107
  55.4 4.8 all-to-all-start.3
  60.2 2.9 copy.60
  63.0 2.2 all-to-all-done.3
  65.2 4.6 all-to-all-start.2
  69.9 9.2 %all-gather = s32[4,1,9]{2,1,0:T(1,128)S(1)} all-gather(s32[1,1,9]{2,1,0:T(1,128)S(1)} %bitcast.123), channel_id=1, replica_groups=mesh['fsdp'=4,'tp'=8] {'fsdp'}, dimensions={0}, use_global_device_ids=true | all-gather | bytes 180 | tf_op jit(solution)/shard_map/all_gather | solution.py:56
  79.2 2.1 constant_dynamic-slice_fusion.1
  81.3 2.9 copy.73
  84.2 0.2 fusion.30
  84.4 0.6 fusion.31
  85.1 2.5 fusion.29
  87.7 34.9 %all-to-all-done.2 = bf16[128,8,1536]{0,2,1:T(8,128)(2,1)} async-done(((bf16[128,8,1536]{0,2,1:T(8,128)(2,1)}), bf16[128,8,1536]{0,2,1:T(8,128)(2,1)}, u32[]{:S(2)}, u32[]{:S(2)}) %all-to-all-start.2) | async-done | bytes 3145760 | tf_op jit(solution)/shard_map/all_to_all | solution.py:26
  122.6 3.9 fusion.7
  126.6 12.5 %fusion.10 = bf16[1536,1024]{1,0:T(8,128)(2,1)S(1)} fusion(bf16[3072,1024]{1,0:T(8,128)(2,1)} %all-gather.4.cloned.1.call-done, s32[1536]{0:T(1024)S(1)} %fusion.27), kind=kOutput, calls=%fused_computation.20 | convolution fusion | flops 9669967872 | bytes 9443328 | tf_op jit(solution)/shard_map/dot_general | solution.py:66
  139.1 1.6 copy-done.8
  140.8 6.9 %convolution_convert_fusion.1 = bf16[1536,1536]{1,0:T(8,128)(2,1)} fusion(bf16[1536,1024]{1,0:T(8,128)(2,1)S(1)} %fusion.10, bf16[1024,1536]{0,1:T(8,128)(2,1)S(1)} %fusion.7), kind=kOutput, calls=%fused_computation.7 | convolution fusion | flops 4834197504 | bytes 11010048 | tf_op jit(solution)/shard_map/dot_general | solution.py:72
  147.7 0.8 copy-done.5
  148.4 0.6 all_to_all.112
  149.1 3.4 all-to-all-start.5
  152.5 2.8 copy.64
  155.3 2.1 all-to-all-done.5
  157.4 4.5 all-to-all-start.4
  161.9 0.3 reduce-scatter.8.cloned.1.call-start
  162.2 2.1 constant_dynamic-slice_fusion
  164.3 2.9 copy.74
  167.2 32.5 %all-to-all-done.4 = bf16[128,8,1536]{0,2,1:T(8,128)(2,1)} async-done(((bf16[128,8,1536]{0,2,1:T(8,128)(2,1)}), bf16[128,8,1536]{0,2,1:T(8,128)(2,1)}, u32[]{:S(2)}, u32[]{:S(2)}) %all-to-all-start.4) | async-done | bytes 3145760 | tf_op jit(solution)/shard_map/all_to_all | solution.py:26
  199.8 4.0 fusion.5
  203.8 6.9 %convolution_convert_fusion = bf16[1536,1536]{1,0:T(8,128)(2,1)} fusion(bf16[1536,1024]{1,0:T(8,128)(2,1)S(1)} %copy-done.9, bf16[1024,1536]{0,1:T(8,128)(2,1)S(1)} %fusion.5), kind=kOutput, calls=%fused_computation.6 | convolution fusion | flops 4834197504 | bytes 11010048 | tf_op jit(solution)/shard_map/dot_general | solution.py:73
  210.7 0.8 copy-done.6
  211.5 7.4 %all_to_all.136 = f32[8,12,128]{2,1,0:T(8,128)S(1)} all-to-all(f32[8,12,128]{2,1,0:T(8,128)S(1)} %all_to_all.119), channel_id=1, replica_groups=mesh['fsdp'=4,'tp'=8] {'tp'}, dimensions={0} | all-to-all | bytes 98304 | tf_op jit(solution)/shard_map/all_to_all | solution.py:30
  218.9 3.7 all-to-all-start.6
  222.7 37.7 %all-to-all-done.6 = bf16[8,1536,128]{2,1,0:T(8,128)(2,1)S(1)} async-done(((bf16[8,1536,128]{2,1,0:T(8,128)(2,1)}), bf16[8,1536,128]{2,1,0:T(8,128)(2,1)S(1)}, u32[]{:S(2)}, u32[]{:S(2)}) %all-to-all-start.6) | async-done | bytes 3145760 | tf_op jit(solution)/shard_map/all_to_all | solution.py:30
  260.3 2.1 copy_bitcast_fusion
  262.5 58.8 %reduce-scatter.8.cloned.1.call-done = bf16[384,1536]{1,0:T(8,128)(2,1)} async-done(((bf16[1536,1536]{1,0:T(8,128)(2,1)}), bf16[384,1536]{1,0:T(8,128)(2,1)}) %reduce-scatter.8.cloned.1.call-update) | async-done | bytes 1179664 | tf_op jit(solution)/shard_map/reduce_scatter | solution.py:76
  321.3 3.4 fusion.16
  324.8 5.1 fusion.9
  329.9 84.9 %all-gather.6.cloned.1.call-done = bf16[1536,1536]{1,0:T(8,128)(2,1)} async-done(((bf16[384,1536]{1,0:T(8,128)(2,1)}), bf16[1536,1536]{1,0:T(8,128)(2,1)}) %all-gather.6.cloned.1.call-update) | async-done | bytes 4718608 | tf_op jit(solution)/shard_map/all_gather | solution.py:81
  414.8 8.1 %convolution_convert_fusion.2 = bf16[1536,1024]{1,0:T(8,128)(2,1)S(1)} fusion(bf16[1536,1536]{1,0:T(8,128)(2,1)} %all-gather.6.cloned.1.call-done, bf16[1536,1024]{1,0:T(8,128)(2,1)} %fusion.9), kind=kOutput, calls=%fused_computation.19 | convolution fusion | flops 4833411072 | bytes 11010048 | tf_op jit(solution)/shard_map/dot_general | solution.py:85
  422.9 3.0 copy.71
  426.0 44.5 %reduce-scatter.10.cloned.1.call-done = bf16[128,1536]{1,0:T(8,128)(2,1)} async-done(((bf16[1024,1536]{1,0:T(8,128)(2,1)}), bf16[128,1536]{1,0:T(8,128)(2,1)}) %reduce-scatter.10.cloned.1.call-update) | async-done | bytes 393232
  470.5 5.5 %fusion.11 = bf16[3008,128]{1,0:T(8,128)(2,1)} fusion(s32[3008]{0:T(1024)S(1)} %select_n.86, bf16[128,1536]{1,0:T(8,128)(2,1)} %reduce-scatter.10.cloned.1.call-done), kind=kOutput, calls=%fused_computation.21 | convolution fusion | flops 1187799040 | bytes 1175296 | tf_op jit(solution)/shard_map/dot_general | solution.py:93
  476.0 4.7 all-to-all-start.8
  480.9 19.5 %all-to-all-done.8 = bf16[4,752,128]{2,1,0:T(8,128)(2,1)S(1)} async-done(((bf16[4,752,128]{2,1,0:T(8,128)(2,1)}), bf16[4,752,128]{2,1,0:T(8,128)(2,1)S(1)}, u32[]{:S(2)}, u32[]{:S(2)}) %all-to-all-start.8) | async-done | bytes 770080 | tf_op jit(solution)/shard_map/all_to_all | solution.py:94
  500.4 1.3 bitcast_select_fusion
  501.7 3.6 all-to-all-start.9
  505.3 1.2 copy.56
  506.4 0.6 slice.17
  507.0 0.6 iota_compare_fusion.13
  507.8 18.0 %all-to-all-done.9 = bf16[8,752,128]{2,1,0:T(8,128)(2,1)S(1)} async-done(((bf16[8,752,128]{2,1,0:T(8,128)(2,1)}), bf16[8,752,128]{2,1,0:T(8,128)(2,1)S(1)}, u32[]{:S(2)}, u32[]{:S(2)}) %all-to-all-start.9) | async-done | bytes 1540128 | tf_op jit(solution)/shard_map/all_to_all | solution.py:100
  526.0 0.5 copy.69
  526.4 1.4 fusion.19
  527.9 1.2 copy.70
  529.0 0.9 convolution_divide_fusion
  (53 shorter events, 1.2 us)
Async XLA Ops:
  9.3 17.8 %all-to-all-start = ((bf16[8,96,512]{2,1,0:T(8,128)(2,1)}), bf16[8,96,512]{2,1,0:T(8,128)(2,1)S(1)}, u32[]{:S(2)}, u32[]{:S(2)}) async-start(bf16[8,96,512]{2,1,0:T(8,128)(2,1)} %bitcast.7), calls=%async_computation | async-start | bytes 1572864 | tf_op jit(solution)/shard_map/all_to_all | solution.py:49
  14.5 112.1 %all-gather.4.cloned.1.call-start = ((), (), s32[]{:S(2)}) async-start(), calls=%async_computation.13 | async-start | bytes 7077888 | tf_op jit(solution)/shard_map/all_gather | solution.py:54
  30.3 24.4 %copy-start.4 = (f32[128,96]{0,1:T(8,128)S(1)}, f32[128,96]{0,1:T(8,128)}, u32[]{:S(2)}) copy-start(f32[128,96]{0,1:T(8,128)} %param.19) | copy-start | bytes 147460
  30.4 29.8 %copy-start.1 = (bf16[128,12288]{1,0:T(8,128)(2,1)S(1)}, bf16[128,12288]{1,0:T(8,128)(2,1)}, u32[]{:S(2)}) copy-start(bf16[128,12288]{1,0:T(8,128)(2,1)} %param.17) | copy-start | bytes 9437188
  55.4 9.8 %all-to-all-start.3 = ((f32[128,8,12]{0,2,1:T(8,128)}), f32[128,8,12]{0,2,1:T(8,128)S(1)}, u32[]{:S(2)}, u32[]{:S(2)}) async-start(f32[128,8,12]{0,2,1:T(8,128)} %all_to_all.107), calls=%async_computation.3 | async-start | bytes 131072 | tf_op jit(solution)/shard_map/all_to_all | solution.py:26
  65.2 4.7 copy-start.7
  65.2 57.4 %all-to-all-start.2 = ((bf16[128,8,1536]{0,2,1:T(8,128)(2,1)}), bf16[128,8,1536]{0,2,1:T(8,128)(2,1)}, u32[]{:S(2)}, u32[]{:S(2)}) async-start(bf16[128,8,1536]{0,2,1:T(8,128)(2,1)} %bitcast.11), calls=%async_computation.2 | async-start | bytes 6291456 | tf_op jit(solution)/shard_map/all_to_all | solution.py:26
  69.8 192.6 %reduce-scatter.6.cloned.1.call-start = ((), (), s32[]{:S(2)}) async-start(), calls=%async_computation.14 | async-start | bytes 5898240 | tf_op jit(solution)/shard_map/reduce_scatter | solution.py:75
  139.1 1.6 copy-start.8
  147.7 0.8 copy-start.5
  147.7 4.8 copy-start.2
  149.1 8.3 %all-to-all-start.5 = ((f32[128,8,12]{0,2,1:T(8,128)}), f32[128,8,12]{0,2,1:T(8,128)S(1)}, u32[]{:S(2)}, u32[]{:S(2)}) async-start(f32[128,8,12]{0,2,1:T(8,128)} %all_to_all.112), calls=%async_computation.6 | async-start | bytes 131072 | tf_op jit(solution)/shard_map/all_to_all | solution.py:26
  157.4 42.4 %all-to-all-start.4 = ((bf16[128,8,1536]{0,2,1:T(8,128)(2,1)}), bf16[128,8,1536]{0,2,1:T(8,128)(2,1)}, u32[]{:S(2)}, u32[]{:S(2)}) async-start(bf16[128,8,1536]{0,2,1:T(8,128)(2,1)} %bitcast.15), calls=%async_computation.5 | async-start | bytes 6291456 | tf_op jit(solution)/shard_map/all_to_all | solution.py:26
  161.9 159.4 %reduce-scatter.8.cloned.1.call-start = ((), (), s32[]{:S(2)}) async-start(), calls=%async_computation.15 | async-start | bytes 5898240 | tf_op jit(solution)/shard_map/reduce_scatter | solution.py:76
  199.8 4.0 copy-start.9
  210.7 0.8 copy-start.6
  218.9 41.4 %all-to-all-start.6 = ((bf16[8,1536,128]{2,1,0:T(8,128)(2,1)}), bf16[8,1536,128]{2,1,0:T(8,128)(2,1)S(1)}, u32[]{:S(2)}, u32[]{:S(2)}) async-start(bf16[8,1536,128]{2,1,0:T(8,128)(2,1)} %bitcast.108), calls=%async_computation.8 | async-start | bytes 6291456 | tf_op jit(solution)/shard_map/all_to_all | solution.py:30
  222.5 192.2 %all-gather.6.cloned.1.call-start = ((), (), s32[]{:S(2)}) async-start(), calls=%async_computation.16 | async-start | bytes 5898240 | tf_op jit(solution)/shard_map/all_gather | solution.py:81
  262.4 62.3 %copy-start = (bf16[1536,1024]{1,0:T(8,128)(2,1)S(1)}, bf16[1536,1024]{1,0:T(8,128)(2,1)}, u32[]{:S(2)}) copy-start(bf16[1536,1024]{1,0:T(8,128)(2,1)} %copy_bitcast_fusion) | copy-start | bytes 9437188
  324.7 145.8 %reduce-scatter.10.cloned.1.call-start = ((), (), s32[]{:S(2)}) async-start(), calls=%async_computation.17 | async-start | bytes 3538944
  476.0 29.2 %copy-start.3 = (bf16[752,512]{1,0:T(8,128)(2,1)S(1)}, bf16[752,512]{1,0:T(8,128)(2,1)}, u32[]{:S(2)}) copy-start(bf16[752,512]{1,0:T(8,128)(2,1)} %param.12) | copy-start | bytes 2310148
  476.0 24.3 %all-to-all-start.8 = ((bf16[4,752,128]{2,1,0:T(8,128)(2,1)}), bf16[4,752,128]{2,1,0:T(8,128)(2,1)S(1)}, u32[]{:S(2)}, u32[]{:S(2)}) async-start(bf16[4,752,128]{2,1,0:T(8,128)(2,1)} %bitcast.23), calls=%async_computation.10 | async-start | bytes 1540096 | tf_op jit(solution)/shard_map/all_to_all | solution.py:94
  501.7 24.2 %all-to-all-start.9 = ((bf16[8,752,128]{2,1,0:T(8,128)(2,1)}), bf16[8,752,128]{2,1,0:T(8,128)(2,1)S(1)}, u32[]{:S(2)}, u32[]{:S(2)}) async-start(bf16[8,752,128]{2,1,0:T(8,128)(2,1)} %bitcast_select_fusion), calls=%async_computation.11 | async-start | bytes 3080192 | tf_op jit(solution)/shard_map/all_to_all | solution.py:100
Sparse Core Ops, SparseCore 0:
  54.9 71.6 all-gather.3
  147.8 85.2 reduce-scatter.5
  235.4 85.7 reduce-scatter.7
  324.8 89.8 all-gather.5
  426.0 44.4 reduce-scatter.9
where the time goes:
time: 538 us; the launch traced here: 536 us
  waiting for transfers between devices  347 us (64%)
  matrix products  40.9 us (8%)
  blocking collectives  38.7 us (7%)
  local copies, waits for them, and re-layouts  35.5 us (7%)
  starting transfers between devices  34.8 us (6%)
  other arithmetic  25.4 us (5%)
  between operations  14.1 us (3%)
    all_gather x1, waiting for transfers between devices, shards(): hidden_all = lax.all_gather(hidden, 'fsdp', axis=0, tiled=True)  84.9 us
    all_to_all x4, waiting for transfers between devices, swap_up(): lax.all_to_all(part, axis_name, split_axis=1, concat_axis=0, tiled=True)  71.8 us
    reduce_scatter x1, waiting for transfers between devices, shards(): up_sum = lax.psum_scatter(up_part, 'fsdp', scatter_dimension=0, tiled=True)  58.8 us
    unnamed x6, waiting for transfers between devices  44.5 us
    all_to_all x1, waiting for transfers between devices, swap_down(): return lax.all_to_all(part, 'tp', split_axis=0, concat_axis=1, tiled=True)  37.7 us
    all_to_all x1, blocking collectives, swap_up(): lax.all_to_all(part, axis_name, split_axis=1, concat_axis=0, tiled=True)  22.1 us
    unnamed x33, local copies, waits for them, and re-layouts  20 us
    all_to_all x1, waiting for transfers between devices, shards(): lax.all_to_all(placed_rows.reshape(groups, cap, narrow), 'fsdp', split_ax...  19.5 us
  transfers between devices with their start and end apart: 13, of which 12 were waited for; matrix products, arithmetic and copies ran while one was open for 8% of the time, Pallas kernels for 0%

commit v1 on v0

v1 whole, which is shorter than its diff:
```python
import functools
import jax
import jax.numpy as jnp
from jax import lax
from jax.experimental import pallas as pl
from jax.experimental.pallas import tpu as pltpu
from jax.sharding import PartitionSpec as P

SEQS = 8
EPSILON = 1e-06
BLOCKS = 2
F32, BF16 = jnp.float32, jnp.bfloat16
MESH = pl.DeviceIdType.MESH


def al(value, size):
    return pl.multiple_of(value, size)


def layer_kernel(n, m, down_here, *refs):
    (x_ref, cg_in, cu_in, st_ref, bg_in, bu_in, cd_in, sd_ref, bd_in, out_ref,
     cg, cu, base, own, got, hid, cd, bd,
     s_code, r_code, s_down, r_down, l_sem, b_sem, s_red, r_red, s_hid, r_hid) = refs
    f, t = lax.axis_index("fsdp"), lax.axis_index("tp")
    kr = cg_in.shape[0]
    depth, units = cg.shape
    cw = base.shape[3]
    chunks = units // cw
    rows = x_ref.shape[0] // BLOCKS
    half = rows // 2
    total = BLOCKS * chunks
    last = n - 1

    barrier = pltpu.get_barrier_semaphore()
    for d in range(1, m):
        pl.semaphore_signal(barrier, inc=1, device_id={"tp": lax.rem(t + d, m)}, device_id_type=MESH)
    for d in range(1, n):
        pl.semaphore_signal(barrier, inc=1, device_id={"fsdp": lax.rem(f + d, n)}, device_id_type=MESH)

    def base_copy(c, slot, which, src):
        return pltpu.make_async_copy(
            src.at[pl.ds(al(f * depth, 16), depth), pl.ds(al(c * cw, 128), cw)],
            base.at[slot, which], b_sem.at[slot, which])

    def base_start(c, slot):
        base_copy(c, slot, 0, bg_in).start()
        base_copy(c, slot, 1, bu_in).start()

    mine = pl.ds(al(t * kr, 16), kr)
    cols = pl.ds(al(t * units, 128), units)
    local = [pltpu.make_async_copy(cg_in.at[:, cols], cg.at[mine, :], l_sem.at[0]),
             pltpu.make_async_copy(cu_in.at[:, cols], cu.at[mine, :], l_sem.at[1]),
             pltpu.make_async_copy(bd_in.at[:, pl.ds(al(f * depth, 128), depth)], bd, l_sem.at[2])]
    if down_here:
        dcw = cd_in.shape[1]
        local.append(pltpu.make_async_copy(
            cd_in.at[pl.ds(al(t * units, 16), units), :], cd.at[:, pl.ds(al(t * dcw, 128), dcw)], l_sem.at[3]))
    else:
        local.append(pltpu.make_async_copy(cd_in, cd, l_sem.at[3]))
    base_start(0, 0)
    for copy in local:
        copy.start()
    pl.semaphore_wait(barrier, m + n - 2)

    def code_copy(c, which, d):
        src, dst = ((cg_in, cg), (cu_in, cu))[which]
        to = lax.rem(t + d, m)
        return pltpu.make_async_remote_copy(
            src_ref=src.at[:, pl.ds(al(to * units + c * cw, 128), cw)],
            dst_ref=dst.at[mine, pl.ds(al(c * cw, 128), cw)],
            send_sem=s_code.at[c, which, d], recv_sem=r_code.at[c, which, d],
            device_id={"tp": to}, device_id_type=MESH)

    def down_copy(d):
        to = lax.rem(t + d, m)
        return pltpu.make_async_remote_copy(
            src_ref=cd_in.at[pl.ds(al(to * units, 16), units), :],
            dst_ref=cd.at[:, pl.ds(al(t * dcw, 128), dcw)],
            send_sem=s_down.at[d], recv_sem=r_down.at[d],
            device_id={"tp": to}, device_id_type=MESH)

    @pl.loop(0, chunks)
    def _(c):
        for d in range(1, m):
            code_copy(c, 0, d).start()
            code_copy(c, 1, d).start()

    if down_here:
        for d in range(1, m):
            down_copy(d).start()
    local[0].wait()
    local[1].wait()

    def unpack(c):
        slot = lax.rem(c, 2)

        @pl.when(c + 1 < chunks)
        def _():
            base_start(c + 1, 1 - slot)
        base_copy(c, slot, 0, bg_in).wait()
        base_copy(c, slot, 1, bu_in).wait()
        for d in range(1, m):
            code_copy(c, 0, d).wait_recv()
            code_copy(c, 1, d).wait_recv()
        here = pl.ds(al(c * cw, 128), cw)
        scales = st_ref[...]
        lane = lax.broadcasted_iota(jnp.int32, scales.shape, 1)
        for which, codes in ((0, cg), (1, cu)):
            picked = jnp.where(lane == c + which * chunks, scales, 0.0)
            column = jnp.sum(picked, axis=1, keepdims=True)
            codes[:, here] = (base[slot, which].astype(F32) + codes[:, here].astype(F32) * column).astype(BF16)

    def partial(k):
        b, c = k // chunks, lax.rem(k, chunks)

        @pl.when(b == 0)
        def _():
            unpack(c)
        here = pl.ds(al(c * cw, 128), cw)
        both = jnp.concatenate([cg[:, here], cu[:, here]], axis=1)
        for side in range(2):
            xs = x_ref[pl.ds(al(b * rows + side * half, 16), half), :]
            own[side, k] = jnp.dot(xs, both, preferred_element_type=F32).astype(BF16)

    def spot(k, side):
        b, c = k // chunks, lax.rem(k, chunks)
        return hid.at[pl.ds(al(b * rows + side * half, 16), half), pl.ds(al(c * cw, 128), cw)]

    def red_copy(k, side):
        return pltpu.make_async_remote_copy(
            src_ref=own.at[side, k], dst_ref=got.at[side, k], send_sem=s_red.at[side, k], recv_sem=r_red.at[side, k],
            device_id={"fsdp": jnp.clip(f + (1 if side else -1), 0, last)}, device_id_type=MESH)

    def hid_copy(k, side):
        return pltpu.make_async_remote_copy(
            src_ref=spot(k, side), dst_ref=spot(k, side), send_sem=s_hid.at[side, k], recv_sem=r_hid.at[side, k],
            device_id={"fsdp": jnp.clip(f + (-1 if side else 1), 0, last)}, device_id_type=MESH)

    def valid(k):
        return (k >= 0) & (k < total)

    def reduce_step(s, side):
        far = f if side else last - f
        k = s - far

        @pl.when(valid(k) & (far > 0))
        def _():
            red_copy(k, side).wait_recv()

            @pl.when(far < last)
            def _():
                own[side, k] = (own[side, k].astype(F32) + got[side, k].astype(F32)).astype(BF16)

            @pl.when(far == last)
            def _():
                both = own[side, k].astype(F32) + got[side, k].astype(F32)
                gate, up = both[:, :cw], both[:, cw:]
                b, c = k // chunks, lax.rem(k, chunks)
                hid[pl.ds(al(b * rows + side * half, 16), half), pl.ds(al(c * cw, 128), cw)] = (
                    jax.nn.silu(gate) * up).astype(BF16)

    def reduce_send(s, side):
        far = f if side else last - f
        k = s - far

        @pl.when(valid(k) & (far < last))
        def _():
            red_copy(k, side).start()

        @pl.when(valid(k) & (far == last))
        def _():
            hid_copy(k, side).start()

    def pass_on(s, side):
        far = f if side else last - f
        k = s - last - (last - far)

        @pl.when(valid(k) & (far < last))
        def _():
            hid_copy(k, side).wait_recv()

            @pl.when(far > 0)
            def _():
                hid_copy(k, side).start()

    partial(0)

    @pl.loop(0, total + 2 * last)
    def _(s):
        for side in range(2):
            reduce_step(s, side)
        for side in range(2):
            reduce_send(s, side)
        for side in range(2):
            pass_on(s, side)

        @pl.when(s + 1 < total)
        def _():
            partial(s + 1)
        done = s - 2 * last

        @pl.when(done == chunks - 1)
        def _():
            local[2].wait()
            local[3].wait()
            if down_here:
                for d in range(1, m):
                    down_copy(d).wait_recv()

            @pl.loop(0, chunks)
            def _(c):
                there = pl.ds(al(c * cw, 16), cw)
                cd[there, :] = (bd[there, :].astype(F32) + cd[there, :].astype(F32) * sd_ref[c]).astype(BF16)

        @pl.when((done >= 0) & (lax.rem(done, chunks) == chunks - 1))
        def _():
            b = done // chunks

            @pl.loop(0, 2)
            def _(side):
                part = pl.ds(al(b * rows + side * half, 16), half)
                out_ref[part, :] = jnp.dot(hid[part, :], cd[...], preferred_element_type=F32).astype(BF16)

    @pl.loop(0, chunks)
    def _(c):
        for d in range(1, m):
            code_copy(c, 0, d).wait_send()
            code_copy(c, 1, d).wait_send()
    if down_here:
        for d in range(1, m):
            down_copy(d).wait_send()

    @pl.loop(0, total)
    def _(k):
        for side in range(2):
            far = f if side else last - f

            @pl.when(far < last)
            def _():
                red_copy(k, side).wait_send()

            @pl.when(far > 0)
            def _():
                hid_copy(k, side).wait_send()


def layer(n, m, x, code_gate, code_up, st, base_gate, base_up, code_down, sd, base_down, down_here):
    rows, depth = x.shape
    units = base_gate.shape[1]
    cw = code_gate.shape[1] // (sd.shape[0] * m)
    chunks = units // cw
    total = BLOCKS * chunks
    half = rows // (2 * BLOCKS)
    anywhere = pl.BlockSpec(memory_space=pl.ANY)
    near = pl.BlockSpec(memory_space=pltpu.VMEM)
    dma = pltpu.SemaphoreType.DMA
    return pl.pallas_call(
        functools.partial(layer_kernel, n, m, down_here),
        out_shape=jax.ShapeDtypeStruct((rows, depth), BF16),
        in_specs=[near, anywhere, anywhere, near, anywhere, anywhere, anywhere, near, anywhere],
        out_specs=near,
        scratch_shapes=[
            pltpu.VMEM((depth, units), BF16), pltpu.VMEM((depth, units), BF16),
            pltpu.VMEM((2, 2, depth, cw), BF16),
            pltpu.VMEM((2, total, half, 2 * cw), BF16), pltpu.VMEM((2, total, half, 2 * cw), BF16),
            pltpu.VMEM((rows, units), BF16),
            pltpu.VMEM((units, depth), BF16), pltpu.VMEM((units, depth), BF16),
            dma((chunks, 2, m)), dma((chunks, 2, m)), dma((m,)), dma((m,)), dma((4,)), dma((2, 2)),
            dma((2, total)), dma((2, total)), dma((2, total)), dma((2, total)),
        ],
        compiler_params=pltpu.CompilerParams(
            collective_id=0, has_side_effects=True, vmem_limit_bytes=67043328),
    )(x, code_gate, code_up, st, base_gate, base_up, code_down, sd, base_down)


def shards(tokens, norm_gain, base_gate, base_up, base_down, code_gate, code_up,
           scale_gate, scale_up, code_down, scale_down, cu_seqlens):
    n, m = lax.axis_size("fsdp"), lax.axis_size("tp")
    me_f, me_t = lax.axis_index("fsdp"), lax.axis_index("tp")
    cap, feat = tokens.shape
    width, units = base_gate.shape
    depth = width // n
    live_all = n * (cap // 2 + SEQS)
    lanes = BLOCKS * m
    rp = live_all // lanes
    ns = -(-(-(-cap // lanes)) // 16) * 16
    kr = code_gate.shape[0]
    nb = scale_gate.shape[1] // m

    bounds_all = lax.all_gather(cu_seqlens, "fsdp", axis=0, tiled=True)
    counts = bounds_all[:, SEQS]
    starts = jnp.cumsum(counts) - counts
    start, live = starts[me_f], counts[me_f]

    q_of = (jnp.arange(m)[:, None] + m * jnp.arange(BLOCKS)[None, :])
    row_of = ((q_of - start) % lanes)[:, :, None] + lanes * jnp.arange(ns)[None, None, :]
    row_of = jnp.where(row_of < live, row_of, -1).reshape(-1)
    slots = jnp.arange(cap, dtype=jnp.int32)
    spread = (row_of[:, None] == slots[None, :]).astype(BF16)
    sent = jnp.dot(spread, tokens, preferred_element_type=F32).astype(BF16)
    wide = lax.all_to_all(sent.reshape(m, BLOCKS * ns, feat), "tp", split_axis=0, concat_axis=0, tiled=True)
    wide = wide.transpose(1, 0, 2).reshape(BLOCKS * ns, width).astype(F32)
    inverse = lax.rsqrt(jnp.mean(wide * wide, axis=1, keepdims=True) + EPSILON)
    normed = (wide * inverse * norm_gain[None, :]).astype(BF16)
    block = lax.all_to_all(normed.reshape(BLOCKS * ns, n, depth), "fsdp", split_axis=1, concat_axis=1, tiled=True)

    q_mine = me_t + m * jnp.arange(BLOCKS)
    r_all = ((q_mine[:, None] - starts[None, :]) % lanes)[:, :, None] + lanes * jnp.arange(ns)[None, None, :]
    slot_all = jnp.where(r_all < counts[None, :, None], (starts[None, :, None] + r_all) // lanes, -1)
    by_group = block.reshape(BLOCKS, ns, n, depth).transpose(0, 2, 1, 3).reshape(BLOCKS, n * ns, depth)
    place = (slot_all.reshape(BLOCKS, 1, n * ns) == jnp.arange(rp)[None, :, None]).astype(BF16)
    mine = jnp.einsum("brk,bkd->brd", place, by_group, preferred_element_type=F32).astype(BF16)
    x = lax.all_gather(mine, "tp", axis=1, tiled=True).reshape(live_all, depth)

    both = jnp.stack([scale_gate.reshape(kr, m, nb), scale_up.reshape(kr, m, nb)], axis=2).reshape(kr, m * 2 * nb)
    st = lax.all_to_all(both, "tp", split_axis=1, concat_axis=0, tiled=True)
    st = jnp.pad(st, ((0, 0), (0, -(2 * nb) % 128)))
    sd = lax.all_to_all(scale_down, "tp", split_axis=0, concat_axis=1, tiled=True)[:, None, :]
    down_here = code_down.shape[1] % 128 == 0
    if not down_here:
        code_down = lax.all_to_all(code_down, "tp", split_axis=0, concat_axis=1, tiled=True)
    out_part = layer(n, m, x, code_gate, code_up, st, base_gate, base_up, code_down, sd, base_down, down_here)

    summed = lax.psum_scatter(out_part.reshape(BLOCKS, m * rp, depth), "tp", scatter_dimension=1, tiled=True)
    back = jnp.einsum("brk,brd->bkd", place, summed, preferred_element_type=F32).astype(BF16)
    back = back.reshape(BLOCKS, n, ns, depth).transpose(1, 0, 2, 3).reshape(n, BLOCKS * ns, depth)
    back = lax.all_to_all(back, "fsdp", split_axis=0, concat_axis=0, tiled=True)
    back = back.transpose(1, 0, 2).reshape(BLOCKS * ns, m, feat).transpose(1, 0, 2)
    back = lax.all_to_all(back, "tp", split_axis=0, concat_axis=0, tiled=True).reshape(m * BLOCKS * ns, feat)
    summed_out = lax.dot_general(spread, back, (((0,), (0,)), ((), ())), preferred_element_type=F32)

    bounds = cu_seqlens[0]
    mixed = (tokens.astype(F32) + summed_out).astype(BF16)
    mixed = jnp.where((slots < live)[:, None], mixed, jnp.zeros((), BF16))
    member = (slots[None, :] >= bounds[:-1, None]) & (slots[None, :] < bounds[1:, None])
    seq_sums = jnp.dot(member.astype(BF16), mixed, preferred_element_type=F32)
    lengths = (bounds[1:] - bounds[:-1]).astype(F32)
    return mixed, seq_sums / lengths[:, None]


def solution(mesh):
    placed = (
        P("fsdp", "tp"), P(), P(None, "tp"), P(None, "tp"), P("tp", None),
        P(("fsdp", "tp"), None), P(("fsdp", "tp"), None),
        P(("fsdp", "tp"), None), P(("fsdp", "tp"), None),
        P(None, ("fsdp", "tp")), P(None, ("fsdp", "tp")), P("fsdp", None),
    )
    return jax.shard_map(shards, mesh=mesh, in_specs=placed,
                         out_specs=(P("fsdp", "tp"), P("fsdp", "tp")), check_vma=False)
```

time: 538 us -> 413 us (0.77)
  waiting for transfers between devices: 347 us -> 112 us
  Pallas kernels: 0 us -> 206 us
  matrix products: 40.9 us -> 7.53 us
  local copies, waits for them, and re-layouts: 35.5 us -> 11.1 us
  other arithmetic: 25.4 us -> 4.66 us
  starting transfers between devices: 34.8 us -> 19.1 us
    pallas_call x0 -> x1, Pallas kernels: none -> 206 us  [layer(): pl.pallas_call(functools.partial(layer_kernel, n, m, down_here), out_shap...]
    all_to_all x8 -> x5, waiting for transfers between devices: 159 us -> 49.8 us  [the longest x1 16.9 us: shards(): lax.all_to_all(normed.reshape(BLOCKS * ns, n, depth), 'fsdp', split_axis=...]
    all_gather x2 -> x1, waiting for transfers between devices: 85 us -> 12.6 us  [shards(): x = lax.all_gather(mine, 'tp', axis=1, tiled=True).reshape(live_all, depth)]
    unnamed x6 -> x2, waiting for transfers between devices: 44.5 us -> 0.03 us
    dot_general x5 -> x4, matrix products: 40 us -> 6.66 us  [the longest x1 2.86 us: shards(): sent = jnp.dot(spread, tokens, preferred_element_type=F32).astype(BF16)]
    unnamed x33 -> x22, local copies, waits for them, and re-layouts: 20 us -> 0.05 us
    convert_element_type x6 -> x1, other arithmetic: 16.7 us -> 0.2 us  [shards(): wide = wide.transpose(1, 0, 2).reshape(BLOCKS * ns, width).astype(F32)]
    all_to_all x8 -> x5, starting transfers between devices: 34.4 us -> 19 us  [the longest x1 4.78 us: shards(): lax.all_to_all(scale_down, 'tp', split_axis=0, concat_axis=1, tiled=True)]
  transfers between devices with their start and end apart: 13 -> 7, of which waited for: 12 -> 7; matrix products, arithmetic and copies ran while one was open for 8% -> 1% of each run, Pallas kernels for 0% -> 0%
where the time goes in v1:
time: 413 us
  Pallas kernels  206 us (50%)
  waiting for transfers between devices  112 us (27%)
  blocking collectives  37.1 us (9%)
  starting transfers between devices  19.1 us (5%)
  between operations  14.3 us (3%)
  local copies, waits for them, and re-layouts  11.1 us (3%)
  matrix products  7.53 us (2%)
  other arithmetic  4.66 us (1%)
    pallas_call x1, Pallas kernels, layer(): pl.pallas_call(functools.partial(layer_kernel, n, m, down_here), out_shap...  206 us
    reduce_scatter x1, waiting for transfers between devices, shards(): lax.psum_scatter(out_part.reshape(BLOCKS, m * rp, depth), 'tp', scatter_d...  49.9 us
    all_to_all x1, blocking collectives, shards(): back = lax.all_to_all(back, 'fsdp', split_axis=0, concat_axis=0, tiled=True)  24.3 us
    all_to_all x1, waiting for transfers between devices, shards(): lax.all_to_all(normed.reshape(BLOCKS * ns, n, depth), 'fsdp', split_axis=...  16.9 us
    all_gather x1, blocking collectives, shards(): bounds_all = lax.all_gather(cu_seqlens, 'fsdp', axis=0, tiled=True)  12.8 us
    all_gather x1, waiting for transfers between devices, shards(): x = lax.all_gather(mine, 'tp', axis=1, tiled=True).reshape(live_all, depth)  12.6 us
    all_to_all x1, waiting for transfers between devices, shards(): lax.all_to_all(sent.reshape(m, BLOCKS * ns, feat), 'tp', split_axis=0, co...  12.5 us
    all_to_all x1, waiting for transfers between devices, shards(): lax.all_to_all(back, 'tp', split_axis=0, concat_axis=0, tiled=True)  11.7 us
  transfers between devices with their start and end apart: 7, of which 7 were waited for; matrix products, arithmetic and copies ran while one was open for 1% of the time, Pallas kernels for 0%

profile of v1, /device:TPU:0, one launch (start us, length us, event | category | flops | bytes accessed | tf_op | source)
XLA Modules:
  0.0 412.5 jit_solution(8532816737863320944)
XLA Ops:
  7.2 12.8 %all-gather = s32[4,1,9]{2,1,0:T(1,128)S(1)} all-gather(s32[1,1,9]{2,1,0:T(1,128)} %bitcast.57), channel_id=1, replica_groups=mesh['fsdp'=4,'tp'=8] {'fsdp'}, dimensions={0}, use_global_device_ids=true | all-gather | bytes 180 | tf_op jit(solution)/shard_map/all_gather | solution.py:290
  20.0 0.2 slice_reduce_fusion
  20.2 0.1 reduce.2
  20.3 0.5 constant_dynamic-slice_fusion
  20.9 0.6 dynamic_slice.7
  21.5 0.7 add_select_fusion
  22.1 0.1 broadcast_add_fusion
  22.2 0.1 add.141
  22.3 0.6 compare_select_fusion
  22.9 0.0 copy-start.7
  22.9 2.9 fusion.3
  25.8 3.9 all-to-all-start
  29.7 12.5 %all-to-all-done = bf16[8,96,512]{2,1,0:T(8,128)(2,1)S(1)} async-done(((bf16[8,96,512]{2,1,0:T(8,128)(2,1)}), bf16[8,96,512]{2,1,0:T(8,128)(2,1)S(1)}, u32[]{:S(2)}, u32[]{:S(2)}) %all-to-all-start) | async-done | bytes 786464 | tf_op jit(solution)/shard_map/all_to_all | solution.py:301
  42.2 0.2 convert_bitcast_fusion
  42.4 0.9 copy.27
  43.4 1.9 reshape.275
  45.3 0.3 fusion.2
  45.6 1.8 multiply_convert_fusion
  47.4 1.1 copy.28
  48.6 3.5 all-to-all-start.1
  52.1 0.0 all-gather.3.cloned.1.call-start
  52.1 0.1 and_select_fusion.1
  52.2 0.1 add.145
  52.3 0.1 add.146
  52.4 0.1 add.151
  52.4 0.1 add.152
  52.5 0.1 lt.72
  52.6 0.1 lt.73
  52.7 0.1 add.148
  52.8 16.9 %all-to-all-done.1 = bf16[96,4,1024]{2,0,1:T(8,128)(2,1)S(1)} async-done(((bf16[96,4,1024]{2,0,1:T(8,128)(2,1)}), bf16[96,4,1024]{2,0,1:T(8,128)(2,1)S(1)}, u32[]{:S(2)}, u32[]{:S(2)}) %all-to-all-start.1) | async-done | bytes 786464 | tf_op jit(solution)/shard_map/all_to_all | solution.py:305
  69.7 0.1 copy.29
  69.7 1.2 convolution_convert_fusion.1
  71.0 0.0 all-gather.3.cloned.1.call-update
  71.0 0.6 all_to_all.44
  71.6 4.8 %all-to-all-start.3 = ((f32[8,12,128]{2,1,0:T(8,128)}), f32[8,12,128]{2,1,0:T(8,128)S(1)}, u32[]{:S(2)}, u32[]{:S(2)}) async-start(f32[8,12,128]{2,1,0:T(8,128)} %all_to_all.44), calls=%async_computation.3 | async-start | bytes 131072 | tf_op jit(solution)/shard_map/all_to_all | solution.py:318
  76.5 0.7 copy.32
  77.2 4.3 %all-to-all-done.3 = f32[8,12,128]{2,1,0:T(8,128)S(1)} async-done(((f32[8,12,128]{2,1,0:T(8,128)}), f32[8,12,128]{2,1,0:T(8,128)S(1)}, u32[]{:S(2)}, u32[]{:S(2)}) %all-to-all-start.3) | async-done | bytes 49184 | tf_op jit(solution)/shard_map/all_to_all | solution.py:318
  81.4 3.4 all-to-all-start.2
  84.8 0.0 reduce-scatter.2.cloned.1.call-start
  84.9 0.6 copy.34
  85.5 4.4 %all-to-all-done.2 = f32[128,8,24]{0,2,1:T(8,128)S(1)} async-done(((f32[128,8,24]{0,2,1:T(8,128)}), f32[128,8,24]{0,2,1:T(8,128)S(1)}, u32[]{:S(2)}, u32[]{:S(2)}) %all-to-all-start.2) | async-done | bytes 98336 | tf_op jit(solution)/shard_map/all_to_all | solution.py:316
  89.9 0.2 copy.33
  90.1 0.8 pad.4.refs_3_
  91.0 12.6 %all-gather.3.cloned.1.call-done = bf16[2,768,1024]{2,1,0:T(8,128)(2,1)} async-done(((bf16[2,96,1024]{2,1,0:T(8,128)(2,1)}), bf16[2,768,1024]{2,1,0:T(8,128)(2,1)}) %all-gather.3.cloned.1.call-update) | async-done | bytes 3145744 | tf_op jit(solution)/shard_map/all_gather | solution.py:313
  103.6 206.2 %shard_map.131 = bf16[1536,1024]{1,0:T(8,128)(2,1)} custom-call(bf16[1536,1024]{1,0:T(8,128)(2,1)} %bitcast.49, bf16[128,12288]{1,0:T(8,128)(2,1)} %refs_1_.1, bf16[128,12288]{1,0:T(8,128)(2,1)} %refs_2_.1, f32[1024,128]{1,0:T(8,128)} %pad.4.refs_3_, bf16[4096,1536]{1,0:T(8,128)(2,1)} %refs_4_.1, bf16[4096,1536]{1,0:T(8,128)(2,1)} %refs_5_.1, ...), custom_call_target="tpu_custom_call" | custom-call | tf_op jit(solution)/shard_map/pallas_call | solution.py:257
  309.8 0.0 reduce-scatter.2.cloned.1.call-update
  309.9 49.9 %reduce-scatter.2.cloned.1.call-done = bf16[2,96,1024]{2,1,0:T(8,128)(2,1)} async-done(((bf16[2,768,1024]{2,1,0:T(8,128)(2,1)}), bf16[2,96,1024]{2,1,0:T(8,128)(2,1)}) %reduce-scatter.2.cloned.1.call-update) | async-done | bytes 393232 | tf_op jit(solution)/shard_map/reduce_scatter | solution.py:324
  359.8 1.4 convolution_convert_fusion
  361.2 0.1 copy.35
  361.2 24.3 %all_to_all.55 = bf16[4,96,1024]{2,1,0:T(8,128)(2,1)S(1)} all-to-all(bf16[4,96,1024]{2,1,0:T(8,128)(2,1)S(1)} %bitcast.46), channel_id=1, replica_groups=mesh['fsdp'=4,'tp'=8] {'fsdp'}, dimensions={0} | all-to-all | bytes 1572864 | tf_op jit(solution)/shard_map/all_to_all | solution.py:327
  385.6 0.6 copy.36
  386.2 0.2 reshape.273
  386.4 0.0 copy-start.6
  386.4 0.0 copy-start.8
  386.4 0.0 copy-start.9
  386.4 1.1 copy.37
  387.5 3.5 all-to-all-start.5
  391.1 0.6 iota_compare_fusion.15
  391.7 0.1 subtract_convert_fusion
  391.8 0.1 slice_bitcast_fusion.1
  391.9 11.7 %all-to-all-done.5 = bf16[8,96,512]{2,1,0:T(8,128)(2,1)S(1)} async-done(((bf16[8,96,512]{2,1,0:T(8,128)(2,1)}), bf16[8,96,512]{2,1,0:T(8,128)(2,1)S(1)}, u32[]{:S(2)}, u32[]{:S(2)}) %all-to-all-start.5) | async-done | bytes 786464 | tf_op jit(solution)/shard_map/all_to_all | solution.py:329
  403.6 1.2 fusion.4
  404.8 0.0 copy-start.10
  404.8 0.9 convolution_divide_fusion
  (30 shorter events, 0.2 us)
Async XLA Ops:
  22.9 2.9 copy-start.7
  25.8 3.9 copy-start.5
  25.8 16.4 %all-to-all-start = ((bf16[8,96,512]{2,1,0:T(8,128)(2,1)}), bf16[8,96,512]{2,1,0:T(8,128)(2,1)S(1)}, u32[]{:S(2)}, u32[]{:S(2)}) async-start(bf16[8,96,512]{2,1,0:T(8,128)(2,1)} %bitcast.4), calls=%async_computation | async-start | bytes 1572864 | tf_op jit(solution)/shard_map/all_to_all | solution.py:301
  48.6 21.1 %all-to-all-start.1 = ((bf16[96,4,1024]{2,0,1:T(8,128)(2,1)}), bf16[96,4,1024]{2,0,1:T(8,128)(2,1)S(1)}, u32[]{:S(2)}, u32[]{:S(2)}) async-start(bf16[96,4,1024]{2,0,1:T(8,128)(2,1)} %copy.28), calls=%async_computation.1 | async-start | bytes 1572864 | tf_op jit(solution)/shard_map/all_to_all | solution.py:305
  52.1 51.5 %all-gather.3.cloned.1.call-start = ((), (), s32[]{:S(2)}) async-start(), calls=%async_computation.7 | async-start | bytes 3538944 | tf_op jit(solution)/shard_map/all_gather | solution.py:313
  52.8 18.2 %copy-start.3 = (s32[2,192]{1,0:T(2,128)}, s32[2,192]{1,0:T(2,128)S(1)}, u32[]{:S(2)}) copy-start(s32[2,192]{1,0:T(2,128)S(1)} %compare_select_fusion.1) | copy-start | bytes 4612
  69.7 1.3 copy-start
  69.7 6.8 %copy-start.1 = (f32[128,96]{0,1:T(8,128)S(1)}, f32[128,96]{0,1:T(8,128)}, u32[]{:S(2)}) copy-start(f32[128,96]{0,1:T(8,128)} %param.19) | copy-start | bytes 147460
  69.7 6.8 %copy-start.2 = (f32[128,96]{0,1:T(8,128)S(1)}, f32[128,96]{0,1:T(8,128)}, u32[]{:S(2)}) copy-start(f32[128,96]{0,1:T(8,128)} %param.20) | copy-start | bytes 147460
  71.6 9.8 %all-to-all-start.3 = ((f32[8,12,128]{2,1,0:T(8,128)}), f32[8,12,128]{2,1,0:T(8,128)S(1)}, u32[]{:S(2)}, u32[]{:S(2)}) async-start(f32[8,12,128]{2,1,0:T(8,128)} %all_to_all.44), calls=%async_computation.3 | async-start | bytes 131072 | tf_op jit(solution)/shard_map/all_to_all | solution.py:318
  81.4 8.5 %all-to-all-start.2 = ((f32[128,8,24]{0,2,1:T(8,128)}), f32[128,8,24]{0,2,1:T(8,128)S(1)}, u32[]{:S(2)}, u32[]{:S(2)}) async-start(f32[128,8,24]{0,2,1:T(8,128)} %copy.32), calls=%async_computation.2 | async-start | bytes 196608 | tf_op jit(solution)/shard_map/all_to_all | solution.py:316
  84.8 275.0 %reduce-scatter.2.cloned.1.call-start = ((), (), s32[]{:S(2)}) async-start(), calls=%async_computation.8 | async-start | bytes 3538944 | tf_op jit(solution)/shard_map/reduce_scatter | solution.py:324
  309.8 49.9 %copy-start.4 = (s32[2,192]{1,0:T(2,128)S(1)}, s32[2,192]{1,0:T(2,128)}, u32[]{:S(2)}) copy-start(s32[2,192]{1,0:T(2,128)} %copy-done.3) | copy-start | bytes 4612
  386.4 5.4 %copy-start.6 = (s32[1,9]{1,0:T(1,128)S(1)}, s32[1,9]{1,0:T(1,128)}, u32[]{:S(2)}) copy-start(s32[1,9]{1,0:T(1,128)} %param.23) | copy-start | bytes 112
  386.4 17.2 %copy-start.8 = (s32[768]{0:T(1024)S(1)}, s32[768]{0:T(1024)}, u32[]{:S(2)}) copy-start(s32[768]{0:T(1024)} %copy-done.7) | copy-start | bytes 9220
  386.4 17.2 %copy-start.9 = (bf16[752,512]{1,0:T(8,128)(2,1)S(1)}, bf16[752,512]{1,0:T(8,128)(2,1)}, u32[]{:S(2)}) copy-start(bf16[752,512]{1,0:T(8,128)(2,1)} %param.12) | copy-start | bytes 2310148
  387.5 16.1 %all-to-all-start.5 = ((bf16[8,96,512]{2,1,0:T(8,128)(2,1)}), bf16[8,96,512]{2,1,0:T(8,128)(2,1)S(1)}, u32[]{:S(2)}, u32[]{:S(2)}) async-start(bf16[8,96,512]{2,1,0:T(8,128)(2,1)} %copy.37), calls=%async_computation.6 | async-start | bytes 1572864 | tf_op jit(solution)/shard_map/all_to_all | solution.py:329
  404.8 0.9 copy-start.10
Sparse Core Ops, SparseCore 0:
  71.1 32.4 all-gather.2
  310.0 49.7 reduce-scatter.1

commit v2 on v1

v2 whole, which is shorter than its diff:
```python
import functools
import jax
import jax.numpy as jnp
from jax import lax
from jax.experimental import pallas as pl
from jax.experimental.pallas import tpu as pltpu
from jax.sharding import PartitionSpec as P

SEQS = 8
EPSILON = 1e-06
BLOCKS = 2
F32, BF16 = jnp.float32, jnp.bfloat16
MESH = pl.DeviceIdType.MESH


def al(value, size):
    return pl.multiple_of(value, size)


def layer_kernel(n, m, here, *refs):
    (sent, gain_ref, row_ref, col_ref, cg_in, cu_in, sg_in, bg_in, bu_in, cd_in, sd_in, bd_in, out_ref,
     cg, cu, base, own, got, hid, cd, bd, x_ref, wide, cut, grp, part_out, part_in, back, back_wide, st, sct, sd,
     s_code, r_code, s_down, r_down, l_sem, b_sem, s_red, r_red, s_hid, r_hid,
     s_tp, r_tp, s_fs, r_fs, s_sc, r_sc) = refs
    f, t = lax.axis_index("fsdp"), lax.axis_index("tp")
    kr = cg_in.shape[0]
    depth, units = cg.shape
    cw = base.shape[3]
    chunks = units // cw
    rows = x_ref.shape[0] // BLOCKS
    half = rows // 2
    rp = rows // m
    ns, feat = sent.shape[2], sent.shape[3]
    nb2 = sg_in.shape[-2]
    total = BLOCKS * chunks
    last = n - 1
    dcw = depth // m

    barrier = pltpu.get_barrier_semaphore()
    for d in range(1, m):
        pl.semaphore_signal(barrier, inc=1, device_id={"tp": lax.rem(t + d, m)}, device_id_type=MESH)
    for d in range(1, n):
        pl.semaphore_signal(barrier, inc=1, device_id={"fsdp": lax.rem(f + d, n)}, device_id_type=MESH)

    def base_copy(c, slot, which, src):
        return pltpu.make_async_copy(
            src.at[pl.ds(al(f * depth, 16), depth), pl.ds(al(c * cw, 128), cw)],
            base.at[slot, which], b_sem.at[slot, which])

    def base_start(c, slot):
        base_copy(c, slot, 0, bg_in).start()
        base_copy(c, slot, 1, bu_in).start()

    mine = pl.ds(al(t * kr, 16), kr)
    cols = pl.ds(al(t * units, 128), units)
    local = [pltpu.make_async_copy(cg_in.at[:, cols], cg.at[mine, :], l_sem.at[0]),
             pltpu.make_async_copy(cu_in.at[:, cols], cu.at[mine, :], l_sem.at[1]),
             pltpu.make_async_copy(bd_in.at[:, pl.ds(al(f * depth, 128), depth)], bd, l_sem.at[2])]
    if here:
        local += [pltpu.make_async_copy(
            cd_in.at[pl.ds(al(t * units, 16), units), :], cd.at[:, pl.ds(al(t * dcw, 128), dcw)], l_sem.at[3]),
            pltpu.make_async_copy(sd_in.at[t], sd.at[:, pl.ds(al(t * dcw, 128), dcw)], l_sem.at[4]),
            pltpu.make_async_copy(sg_in.at[t], sct.at[0:nb2, pl.ds(al(t * kr, 128), kr)], l_sem.at[5])]
    else:
        local += [pltpu.make_async_copy(cd_in, cd, l_sem.at[3]), pltpu.make_async_copy(sd_in, sd, l_sem.at[4]),
                  pltpu.make_async_copy(sg_in, sct.at[0:nb2, :], l_sem.at[5])]
    base_start(0, 0)
    if nb2 < sct.shape[0]:
        sct[nb2:, :] = jnp.zeros_like(sct[nb2:, :])
    for copy in local:
        copy.start()

    def to_tp(b, stage, d, src, dst):
        return pltpu.make_async_remote_copy(
            src_ref=src, dst_ref=dst, send_sem=s_tp.at[stage, b, d], recv_sem=r_tp.at[stage, b, d],
            device_id={"tp": lax.rem(t + d, m)}, device_id_type=MESH)

    def to_fs(b, stage, d, src, dst):
        return pltpu.make_async_remote_copy(
            src_ref=src, dst_ref=dst, send_sem=s_fs.at[stage, b, d], recv_sem=r_fs.at[stage, b, d],
            device_id={"fsdp": lax.rem(f + d, n)}, device_id_type=MESH)

    my_feat = pl.ds(al(t * feat, 128), feat)
    my_depth = pl.ds(al(f * depth, 128), depth)

    def my_part(b):
        return pl.ds(al(b * rows + t * rp, 16), rp)

    def rows_out(b, d):
        return to_tp(b, 0, d, sent.at[lax.rem(t + d, m), b], wide.at[b, :, my_feat])

    def normed_out(b, d):
        return to_fs(b, 0, d, cut.at[b, lax.rem(f + d, n)], grp.at[b, pl.ds(al(f * ns, 16), ns), :])

    def x_out(b, d):
        return to_tp(b, 1, d, x_ref.at[my_part(b), :], x_ref.at[my_part(b), :])

    def sum_out(b, d):
        return to_tp(b, 2, d, part_out.at[b, lax.rem(t + d, m)], part_in.at[b, t])

    def back_out(b, d):
        return to_fs(b, 1, d, back.at[b, lax.rem(f + d, n)], back_wide.at[b, :, my_depth])

    def home_out(b, d):
        return to_tp(b, 3, d, back_wide.at[b, :, pl.ds(al(lax.rem(t + d, m) * feat, 128), feat)], out_ref.at[t, b])

    def scale_copy(d):
        to = lax.rem(t + d, m)
        return pltpu.make_async_remote_copy(
            src_ref=sg_in.at[to], dst_ref=sct.at[0:nb2, pl.ds(al(t * kr, 128), kr)],
            send_sem=s_sc.at[0, d], recv_sem=r_sc.at[0, d], device_id={"tp": to}, device_id_type=MESH)

    def scale_down_copy(d):
        to = lax.rem(t + d, m)
        return pltpu.make_async_remote_copy(
            src_ref=sd_in.at[to], dst_ref=sd.at[:, pl.ds(al(t * dcw, 128), dcw)],
            send_sem=s_sc.at[1, d], recv_sem=r_sc.at[1, d], device_id={"tp": to}, device_id_type=MESH)

    def code_copy(c, which, d):
        src, dst = ((cg_in, cg), (cu_in, cu))[which]
        to = lax.rem(t + d, m)
        return pltpu.make_async_remote_copy(
            src_ref=src.at[:, pl.ds(al(to * units + c * cw, 128), cw)],
            dst_ref=dst.at[mine, pl.ds(al(c * cw, 128), cw)],
            send_sem=s_code.at[c, which, d], recv_sem=r_code.at[c, which, d],
            device_id={"tp": to}, device_id_type=MESH)

    def down_copy(d):
        to = lax.rem(t + d, m)
        return pltpu.make_async_remote_copy(
            src_ref=cd_in.at[pl.ds(al(to * units, 16), units), :],
            dst_ref=cd.at[:, pl.ds(al(t * dcw, 128), dcw)],
            send_sem=s_down.at[d], recv_sem=r_down.at[d],
            device_id={"tp": to}, device_id_type=MESH)

    def codes_start(first, stop):
        @pl.loop(first, stop)
        def _(c):
            for d in range(1, m):
                code_copy(c, 0, d).start()
                code_copy(c, 1, d).start()

    def normalise(b):
        for d in range(1, m):
            rows_out(b, d).wait_recv()
        values = wide[b].astype(F32)
        inverse = lax.rsqrt(jnp.mean(values * values, axis=1, keepdims=True) + EPSILON)
        normed = (values * inverse * gain_ref[...]).astype(BF16)
        for j in range(n):
            cut[b, j] = normed[:, j * depth:(j + 1) * depth]
        grp[b, pl.ds(al(f * ns, 16), ns), :] = cut[b, f]
        for d in range(1, n):
            normed_out(b, d).start()

    def gather(b):
        for d in range(1, n):
            normed_out(b, d).wait_recv()
        place = lax.broadcasted_iota(jnp.int32, (rp, n * ns), 0) == row_ref[b]
        place = jnp.where(place, 1.0, 0.0).astype(BF16)
        x_ref[my_part(b), :] = jnp.dot(place, grp[b], preferred_element_type=F32).astype(BF16)
        for d in range(1, m):
            x_out(b, d).start()

    pl.semaphore_wait(barrier, m + n - 2)
    for b in range(BLOCKS):
        for d in range(1, m):
            rows_out(b, d).start()
    if here:
        for d in range(1, m):
            scale_copy(d).start()
    early = min(2, chunks)
    codes_start(0, early)
    for b in range(BLOCKS):
        wide[b, :, my_feat] = sent[t, b]
    for b in range(BLOCKS):
        normalise(b)
    gather(0)
    codes_start(early, chunks)
    local[5].wait()
    if here:
        for d in range(1, m):
            scale_copy(d).wait_recv()
    for j in range(depth // 128):
        st[j * 128:(j + 1) * 128, :] = sct[:, j * 128:(j + 1) * 128].T
    for b in range(1, BLOCKS):
        gather(b)
    if here:
        for d in range(1, m):
            scale_down_copy(d).start()
            down_copy(d).start()
    local[0].wait()
    local[1].wait()

    def unpack(c):
        slot = lax.rem(c, 2)

        @pl.when(c + 1 < chunks)
        def _():
            base_start(c + 1, 1 - slot)
        base_copy(c, slot, 0, bg_in).wait()
        base_copy(c, slot, 1, bu_in).wait()
        for d in range(1, m):
            code_copy(c, 0, d).wait_recv()
            code_copy(c, 1, d).wait_recv()
        there = pl.ds(al(c * cw, 128), cw)
        scales = st[...]
        lane = lax.broadcasted_iota(jnp.int32, scales.shape, 1)
        for which, codes in ((0, cg), (1, cu)):
            picked = jnp.where(lane == c + which * chunks, scales, 0.0)
            column = jnp.sum(picked, axis=1, keepdims=True)
            codes[:, there] = (base[slot, which].astype(F32) + codes[:, there].astype(F32) * column).astype(BF16)

    def partial(k):
        b, c = k // chunks, lax.rem(k, chunks)

        @pl.when(c == 0)
        def _():
            for d in range(1, m):
                x_out(b, d).wait_recv()

        @pl.when(b == 0)
        def _():
            unpack(c)
        there = pl.ds(al(c * cw, 128), cw)
        both = jnp.concatenate([cg[:, there], cu[:, there]], axis=1)
        for side in range(2):
            xs = x_ref[pl.ds(al(b * rows + side * half, 16), half), :]
            own[side, k] = jnp.dot(xs, both, preferred_element_type=F32).astype(BF16)

    def spot(k, side):
        b, c = k // chunks, lax.rem(k, chunks)
        return hid.at[pl.ds(al(b * rows + side * half, 16), half), pl.ds(al(c * cw, 128), cw)]

    def red_copy(k, side):
        return pltpu.make_async_remote_copy(
            src_ref=own.at[side, k], dst_ref=got.at[side, k], send_sem=s_red.at[side, k], recv_sem=r_red.at[side, k],
            device_id={"fsdp": jnp.clip(f + (1 if side else -1), 0, last)}, device_id_type=MESH)

    def hid_copy(k, side):
        return pltpu.make_async_remote_copy(
            src_ref=spot(k, side), dst_ref=spot(k, side), send_sem=s_hid.at[side, k], recv_sem=r_hid.at[side, k],
            device_id={"fsdp": jnp.clip(f + (-1 if side else 1), 0, last)}, device_id_type=MESH)

    def valid(k):
        return (k >= 0) & (k < total)

    def reduce_step(s, side):
        far = f if side else last - f
        k = s - far

        @pl.when(valid(k) & (far > 0))
        def _():
            red_copy(k, side).wait_recv()

            @pl.when(far < last)
            def _():
                own[side, k] = (own[side, k].astype(F32) + got[side, k].astype(F32)).astype(BF16)

            @pl.when(far == last)
            def _():
                both = own[side, k].astype(F32) + got[side, k].astype(F32)
                gate, up = both[:, :cw], both[:, cw:]
                b, c = k // chunks, lax.rem(k, chunks)
                hid[pl.ds(al(b * rows + side * half, 16), half), pl.ds(al(c * cw, 128), cw)] = (
                    jax.nn.silu(gate) * up).astype(BF16)

    def reduce_send(s, side):
        far = f if side else last - f
        k = s - far

        @pl.when(valid(k) & (far < last))
        def _():
            red_copy(k, side).start()

        @pl.when(valid(k) & (far == last))
        def _():
            hid_copy(k, side).start()

    def pass_on(s, side):
        far = f if side else last - f
        k = s - last - (last - far)

        @pl.when(valid(k) & (far < last))
        def _():
            hid_copy(k, side).wait_recv()

            @pl.when(far > 0)
            def _():
                hid_copy(k, side).start()

    def down_weights():
        for i in range(2, 5):
            local[i].wait()
        if here:
            for d in range(1, m):
                scale_down_copy(d).wait_recv()
                down_copy(d).wait_recv()

        @pl.loop(0, chunks)
        def _(c):
            there = pl.ds(al(c * cw, 16), cw)
            cd[there, :] = (bd[there, :].astype(F32) + cd[there, :].astype(F32) * sd[pl.ds(c, 1), :]).astype(BF16)

    def down(b):
        for j in reversed(range(m // 2)):
            first = lax.rem(t // 2 + j, m // 2) * 2
            both = jnp.dot(hid[pl.ds(al(b * rows + first * rp, 16), 2 * rp), :], cd[...], preferred_element_type=F32)
            both = both.astype(BF16)
            part_out[b, first] = both[:rp]
            part_out[b, first + 1] = both[rp:]
            for e in range(2):
                d = lax.rem(first + e - t + m, m)
                if j:
                    sum_out(b, d).start()
                else:
                    @pl.when(d > 0)
                    def _():
                        sum_out(b, d).start()

    def send_back(b):
        acc = part_out[b, t].astype(F32)
        for d in range(1, m):
            sum_out(b, d).wait_recv()
        for d in range(1, m):
            acc = acc + part_in[b, lax.rem(t + d, m)].astype(F32)
        place = lax.broadcasted_iota(jnp.int32, (n * ns, rp), 1) == col_ref[b]
        place = jnp.where(place, 1.0, 0.0).astype(BF16)
        spread = jnp.dot(place, acc.astype(BF16), preferred_element_type=F32).astype(BF16)
        for g in range(n):
            back[b, g] = spread[g * ns:(g + 1) * ns]
        for d in range(1, n):
            back_out(b, d).start()
        back_wide[b, :, my_depth] = back[b, f]

    def send_home(b):
        for d in range(1, n):
            back_out(b, d).wait_recv()
        for d in range(1, m):
            home_out(b, d).start()
        out_ref[t, b] = back_wide[b, :, my_feat]

    steps = total + 2 * last
    tasks = [(chunks - 1 + 2 * last, down_weights)]
    for b in range(BLOCKS):
        at = (b + 1) * chunks - 1 + 2 * last
        tasks += [(at, functools.partial(down, b)), (at + 4, functools.partial(send_back, b)),
                  (at + 6, functools.partial(send_home, b))]

    partial(0)

    @pl.loop(0, steps)
    def _(s):
        for side in range(2):
            reduce_step(s, side)
        for side in range(2):
            reduce_send(s, side)
        for side in range(2):
            pass_on(s, side)

        @pl.when(s + 1 < total)
        def _():
            partial(s + 1)
        for at, task in tasks:
            if at < steps:
                pl.when(s == at)(task)

    for at, task in tasks:
        if at >= steps:
            task()
    for b in range(BLOCKS):
        for d in range(1, m):
            home_out(b, d).wait_recv()

    @pl.loop(0, chunks)
    def _(c):
        for d in range(1, m):
            code_copy(c, 0, d).wait_send()
            code_copy(c, 1, d).wait_send()
    if here:
        for d in range(1, m):
            down_copy(d).wait_send()
            scale_copy(d).wait_send()
            scale_down_copy(d).wait_send()
    for b in range(BLOCKS):
        for d in range(1, m):
            for out in (rows_out, x_out, sum_out, home_out):
                out(b, d).wait_send()
        for d in range(1, n):
            for out in (normed_out, back_out):
                out(b, d).wait_send()

    @pl.loop(0, total)
    def _(k):
        for side in range(2):
            far = f if side else last - f

            @pl.when(far < last)
            def _():
                red_copy(k, side).wait_send()

            @pl.when(far > 0)
            def _():
                hid_copy(k, side).wait_send()


def layer(n, m, here, sent, gain, row_of, col_of, code_gate, code_up, scales, base_gate, base_up,
          code_down, scale_down, base_down, live_all):
    width, units = base_gate.shape
    depth = width // n
    ns, feat = sent.shape[2:]
    chunks = scale_down.shape[-2]
    cw = units // chunks
    total = BLOCKS * chunks
    half = live_all // (2 * BLOCKS)
    rp = live_all // (BLOCKS * m)
    anywhere = pl.BlockSpec(memory_space=pl.ANY)
    near = pl.BlockSpec(memory_space=pltpu.VMEM)
    dma = pltpu.SemaphoreType.DMA
    vm = pltpu.VMEM
    return pl.pallas_call(
        functools.partial(layer_kernel, n, m, here),
        out_shape=jax.ShapeDtypeStruct((m, BLOCKS, ns, feat), BF16),
        in_specs=[near, near, near, near] + [anywhere] * 8,
        out_specs=near,
        scratch_shapes=[
            vm((depth, units), BF16), vm((depth, units), BF16), vm((2, 2, depth, cw), BF16),
            vm((2, total, half, 2 * cw), BF16), vm((2, total, half, 2 * cw), BF16),
            vm((live_all, units), BF16), vm((units, depth), BF16), vm((units, depth), BF16),
            vm((live_all, depth), BF16), vm((BLOCKS, ns, width), BF16), vm((BLOCKS, n, ns, depth), BF16),
            vm((BLOCKS, n * ns, depth), BF16), vm((BLOCKS, m, rp, depth), BF16), vm((BLOCKS, m, rp, depth), BF16),
            vm((BLOCKS, n, ns, depth), BF16), vm((BLOCKS, ns, width), BF16),
            vm((depth, 128), F32), vm((128, depth), F32), vm((chunks, depth), F32),
            dma((chunks, 2, m)), dma((chunks, 2, m)), dma((m,)), dma((m,)), dma((6,)), dma((2, 2)),
            dma((2, total)), dma((2, total)), dma((2, total)), dma((2, total)),
            dma((4, BLOCKS, m)), dma((4, BLOCKS, m)), dma((2, BLOCKS, n)), dma((2, BLOCKS, n)), dma((2, m)), dma((2, m)),
        ],
        compiler_params=pltpu.CompilerParams(
            collective_id=0, has_side_effects=True, vmem_limit_bytes=67043328),
    )(sent, gain, row_of, col_of, code_gate, code_up, scales, base_gate, base_up, code_down, scale_down, base_down)


def shards(tokens, norm_gain, base_gate, base_up, base_down, code_gate, code_up,
           scale_gate, scale_up, code_down, scale_down, cu_seqlens):
    n, m = lax.axis_size("fsdp"), lax.axis_size("tp")
    me_f, me_t = lax.axis_index("fsdp"), lax.axis_index("tp")
    cap, feat = tokens.shape
    live_all = n * (cap // 2 + SEQS)
    lanes = BLOCKS * m
    rp = live_all // lanes
    ns = -(-(-(-cap // lanes)) // 16) * 16
    kr = code_gate.shape[0]
    nb = scale_gate.shape[1] // m

    bounds_all = lax.all_gather(cu_seqlens, "fsdp", axis=0, tiled=True)
    counts = bounds_all[:, SEQS]
    starts = jnp.cumsum(counts) - counts
    start, live = starts[me_f], counts[me_f]

    q_of = (jnp.arange(m)[:, None] + m * jnp.arange(BLOCKS)[None, :])
    row_of = ((q_of - start) % lanes)[:, :, None] + lanes * jnp.arange(ns)[None, None, :]
    row_of = jnp.where(row_of < live, row_of, -1).reshape(-1)
    slots = jnp.arange(cap, dtype=jnp.int32)
    spread = (row_of[:, None] == slots[None, :]).astype(BF16)
    sent = jnp.dot(spread, tokens, preferred_element_type=F32).astype(BF16)

    q_mine = me_t + m * jnp.arange(BLOCKS)
    r_all = ((q_mine[:, None] - starts[None, :]) % lanes)[:, :, None] + lanes * jnp.arange(ns)[None, None, :]
    slot_all = jnp.where(r_all < counts[None, :, None], (starts[None, :, None] + r_all) // lanes, -1)
    slot_all = slot_all.reshape(BLOCKS, n * ns)

    scales = jnp.concatenate([scale_gate.reshape(kr, m, nb), scale_up.reshape(kr, m, nb)], axis=2).transpose(1, 2, 0)
    scales = jnp.pad(scales, ((0, 0), (0, -(2 * nb) % 8), (0, 0)))
    scale_down = scale_down.reshape(m, nb, -1)
    here = code_down.shape[1] % 128 == 0 and kr % 128 == 0
    if not here:
        code_down = lax.all_to_all(code_down, "tp", split_axis=0, concat_axis=1, tiled=True)
        scales = lax.all_to_all(scales, "tp", split_axis=0, concat_axis=2, tiled=True)[0]
        scale_down = lax.all_to_all(scale_down, "tp", split_axis=0, concat_axis=2, tiled=True)[0]
    home = layer(n, m, here, sent.reshape(m, BLOCKS, ns, feat), norm_gain[None, :], slot_all[:, None, :],
                 slot_all[:, :, None], code_gate, code_up, scales, base_gate, base_up, code_down, scale_down,
                 base_down, live_all)
    summed_out = lax.dot_general(spread, home.reshape(m * BLOCKS * ns, feat), (((0,), (0,)), ((), ())),
                                 preferred_element_type=F32)

    bounds = cu_seqlens[0]
    mixed = (tokens.astype(F32) + summed_out).astype(BF16)
    mixed = jnp.where((slots < live)[:, None], mixed, jnp.zeros((), BF16))
    member = (slots[None, :] >= bounds[:-1, None]) & (slots[None, :] < bounds[1:, None])
    seq_sums = jnp.dot(member.astype(BF16), mixed, preferred_element_type=F32)
    lengths = (bounds[1:] - bounds[:-1]).astype(F32)
    return mixed, seq_sums / lengths[:, None]


def solution(mesh):
    placed = (
        P("fsdp", "tp"), P(), P(None, "tp"), P(None, "tp"), P("tp", None),
        P(("fsdp", "tp"), None), P(("fsdp", "tp"), None),
        P(("fsdp", "tp"), None), P(("fsdp", "tp"), None),
        P(None, ("fsdp", "tp")), P(None, ("fsdp", "tp")), P("fsdp", None),
    )
    return jax.shard_map(shards, mesh=mesh, in_specs=placed,
                         out_specs=(P("fsdp", "tp"), P("fsdp", "tp")), check_vma=False)
```

time: 413 us -> 295 us (0.71)
  waiting for transfers between devices: 112 us -> 0 us
  Pallas kernels: 206 us -> 266 us
  blocking collectives: 37.1 us -> 12.9 us
  starting transfers between devices: 19.1 us -> 0 us
  between operations: 14.3 us -> 0.77 us
  local copies, waits for them, and re-layouts: 11.1 us -> 2.76 us
    pallas_call x1, Pallas kernels: 206 us -> 266 us  [layer(): pl.pallas_call(functools.partial(layer_kernel, n, m, here), out_shape=jax...]
    reduce_scatter x1 -> x0, waiting for transfers between devices: 49.9 us -> none  [shards(): lax.psum_scatter(out_part.reshape(BLOCKS, m * rp, depth), 'tp', scatter_d...]
    all_to_all x5 -> x0, waiting for transfers between devices: 49.8 us -> none  [the longest x1 16.9 us: shards(): lax.all_to_all(normed.reshape(BLOCKS * ns, n, depth), 'fsdp', split_axis=...]
    all_to_all x1 -> x0, blocking collectives: 24.3 us -> none  [shards(): back = lax.all_to_all(back, 'fsdp', split_axis=0, concat_axis=0, tiled=True)]
    all_to_all x5 -> x0, starting transfers between devices: 19 us -> none  [the longest x1 4.78 us: shards(): lax.all_to_all(scale_down, 'tp', split_axis=0, concat_axis=1, tiled=True)]
    all_gather x1 -> x0, waiting for transfers between devices: 12.6 us -> none  [shards(): x = lax.all_gather(mine, 'tp', axis=1, tiled=True).reshape(live_all, depth)]
  transfers between devices with their start and end apart: 7 -> 0, of which waited for: 7 -> 0; matrix products, arithmetic and copies ran while one was open for 1% -> 0% of each run, Pallas kernels for 0% -> 0%
where the time goes in v2:
time: 295 us; the launch traced here: 293 us
  Pallas kernels  266 us (90%)
  blocking collectives  12.9 us (4%)
  matrix products  6.28 us (2%)
  other arithmetic  4.31 us (1%)
    pallas_call x1, Pallas kernels, layer(): pl.pallas_call(functools.partial(layer_kernel, n, m, here), out_shape=jax...  266 us
    all_gather x1, blocking collectives, shards(): bounds_all = lax.all_gather(cu_seqlens, 'fsdp', axis=0, tiled=True)  12.9 us

profile of v2, /device:TPU:0, one launch (start us, length us, event | category | flops | bytes accessed | tf_op | source)
XLA Modules:
  0.0 293.3 jit_solution(14866980538642323856)
XLA Ops:
  0.6 0.0 copy-start
  0.6 0.0 copy-start.1
  0.7 12.9 %all-gather = s32[4,1,9]{2,1,0:T(1,128)S(1)} all-gather(s32[1,1,9]{2,1,0:T(1,128)} %bitcast.28), channel_id=1, replica_groups=mesh['fsdp'=4,'tp'=8] {'fsdp'}, dimensions={0}, use_global_device_ids=true | all-gather | bytes 180 | tf_op jit(solution)/shard_map/all_gather | solution.py:454
  13.6 0.2 slice_reduce_fusion
  13.8 0.1 reduce
  13.9 0.6 dynamic_slice.7
  14.5 0.7 add_select_fusion.1
  15.2 0.1 broadcast_add_fusion
  15.3 0.1 add.170
  15.4 0.5 constant_dynamic-slice_fusion
  15.9 0.6 compare_select_fusion
  16.4 0.0 copy-start.4
  16.4 0.0 copy-start.2
  16.4 2.9 fusion.2
  19.3 0.1 and_select_fusion.1
  19.4 0.0 copy-done.4
  19.4 0.1 add.174
  19.5 0.1 add.190
  19.6 0.1 add.180
  19.7 0.1 add.181
  19.7 0.1 lt.86
  19.8 0.1 lt.87
  19.9 0.1 add.177
  20.0 0.9 fusion.7.refs_3_
  20.9 0.1 add.175
  21.0 0.6 compare_select_fusion.1.refs_2_
  21.6 0.0 copy-done
  21.6 0.0 copy-done.1
  21.6 0.6 maximum_bitcast_fusion.refs_6_
  22.2 0.0 copy-done.2
  22.3 0.6 reshape.441.refs_10_
  22.9 266.3 %shard_map.131 = bf16[8,2,48,512]{3,2,1,0:T(8,128)(2,1)} custom-call(bf16[8,2,48,512]{3,2,1,0:T(8,128)(2,1)} %bitcast.24, f32[1,4096]{1,0:T(1,128)} %bitcast.26, s32[2,1,192]{2,1,0:T(1,128)} %compare_select_fusion.1.refs_2_, s32[2,192,1]{2,1,0:T(8,128)} %fusion.7.refs_3_, bf16[128,12288]{1,0:T(8,128)(2,1)} %refs_4_.1, bf16[128,12288]{1,0:T(8,128)(2,1)} %refs_5_.1, ...), custom_call_target="tpu_custom_call" | custom-call | tf_op jit(solution)/shard_map/pallas_call | solution.py:420
  289.1 0.0 copy-start.3
  289.2 0.6 iota_compare_fusion.12
  289.7 2.6 fusion.3
  292.3 0.0 copy-done.3
  292.3 0.0 copy-start.5
  292.3 0.1 slice_bitcast_fusion.1
  292.4 0.1 subtract_convert_fusion
  292.5 0.9 convolution_divide_fusion
  293.3 0.0 copy-done.5
  (8 shorter events, 0.1 us)
Async XLA Ops:
  0.6 20.9 %copy-start = (f32[128,96]{0,1:T(8,128)S(1)}, f32[128,96]{0,1:T(8,128)}, u32[]{:S(2)}) copy-start(f32[128,96]{0,1:T(8,128)} %param.19) | copy-start | bytes 147460
  0.6 20.9 %copy-start.1 = (f32[128,96]{0,1:T(8,128)S(1)}, f32[128,96]{0,1:T(8,128)}, u32[]{:S(2)}) copy-start(f32[128,96]{0,1:T(8,128)} %param.20) | copy-start | bytes 147460
  16.4 3.0 %copy-start.4 = (s32[768]{0:T(1024)}, s32[768]{0:T(1024)S(1)}, u32[]{:S(2)}) copy-start(s32[768]{0:T(1024)S(1)} %compare_select_fusion) | copy-start | bytes 9220
  16.4 5.8 %copy-start.2 = (f32[96,128]{1,0:T(8,128)S(1)}, f32[96,128]{1,0:T(8,128)}, u32[]{:S(2)}) copy-start(f32[96,128]{1,0:T(8,128)} %param.22) | copy-start | bytes 147460
  289.1 3.1 %copy-start.3 = (s32[1,9]{1,0:T(1,128)S(1)}, s32[1,9]{1,0:T(1,128)}, u32[]{:S(2)}) copy-start(s32[1,9]{1,0:T(1,128)} %param.23) | copy-start | bytes 112
  292.3 1.0 copy-start.5

commit v3 on v2

--- a/solution.py
+++ b/solution.py
@@ -9,6 +9,7 @@
 SEQS = 8
 EPSILON = 1e-06
 BLOCKS = 2
+SUB = 2
 F32, BF16 = jnp.float32, jnp.bfloat16
 MESH = pl.DeviceIdType.MESH
 
@@ -20,7 +21,7 @@
 def layer_kernel(n, m, here, *refs):
     (sent, gain_ref, row_ref, col_ref, cg_in, cu_in, sg_in, bg_in, bu_in, cd_in, sd_in, bd_in, out_ref,
      cg, cu, base, own, got, hid, cd, bd, x_ref, wide, cut, grp, part_out, part_in, back, back_wide, st, sct, sd,
-     s_code, r_code, s_down, r_down, l_sem, b_sem, s_red, r_red, s_hid, r_hid,
+     s_code, r_code, s_down, r_down, l_sem, b_sem, s_red, r_red, s_hid, r_hid, s_x, r_x,
      s_tp, r_tp, s_fs, r_fs, s_sc, r_sc) = refs
     f, t = lax.axis_index("fsdp"), lax.axis_index("tp")
     kr = cg_in.shape[0]
@@ -92,8 +93,54 @@
     def normed_out(b, d):
         return to_fs(b, 0, d, cut.at[b, lax.rem(f + d, n)], grp.at[b, pl.ds(al(f * ns, 16), ns), :])
 
-    def x_out(b, d):
-        return to_tp(b, 1, d, x_ref.at[my_part(b), :], x_ref.at[my_part(b), :])
+    def flip(bits):
+        peer, bit = t, 1
+        while bit <= bits:
+            if bits & bit:
+                peer = peer + bit - 2 * bit * lax.rem(t // bit, 2)
+            bit *= 2
+        return peer
+
+    def x_copy(b, h, mask, bit):
+        spot = x_ref.at[pl.ds(al(b * rows + flip(mask) * rp + h * (rp // 2), 16), rp // 2), :]
+        return pltpu.make_async_remote_copy(
+            src_ref=spot, dst_ref=spot, send_sem=s_x.at[b, h, mask ^ bit], recv_sem=r_x.at[b, h, mask ^ bit],
+            device_id={"tp": flip(bit)}, device_id_type=MESH)
+
+    def x_arrived(b, h, mask):
+        spot = x_ref.at[pl.ds(al(b * rows + flip(mask) * rp + h * (rp // 2), 16), rp // 2), :]
+        pltpu.make_async_remote_copy(
+            src_ref=spot, dst_ref=spot, send_sem=s_x.at[b, h, mask], recv_sem=r_x.at[b, h, mask],
+            device_id={"tp": flip(1)}, device_id_type=MESH).wait_recv()
+
+    far_bits = [2 ** i for i in range(1, m.bit_length() - 1)]
+    far_masks = sorted(range(2, m, 2), key=lambda mask: (bin(mask).count("1"), mask))
+    orders = (far_bits, far_bits[::-1])
+
+    def onward(h, mask):
+        order = orders[h]
+        used = [i for i, bit in enumerate(order) if mask & bit]
+        return order[max(used, default=-1) + 1:]
+
+    def relay(b, phase):
+        for mask in [0] + far_masks:
+            if bin(mask).count("1") == phase:
+                for h in range(2):
+                    if mask:
+                        x_arrived(b, h, mask)
+                    for bit in onward(h, mask) + [1]:
+                        x_copy(b, h, mask, bit).start()
+
+    def x_wait(b):
+        for mask in range(1, m, 2):
+            for h in range(2):
+                x_arrived(b, h, mask)
+
+    def x_sent(b):
+        for mask in [0] + far_masks:
+            for h in range(2):
+                for bit in onward(h, mask) + [1]:
+                    x_copy(b, h, mask, bit).wait_send()
 
     def sum_out(b, d):
         return to_tp(b, 2, d, part_out.at[b, lax.rem(t + d, m)], part_in.at[b, t])
@@ -133,12 +180,10 @@
             send_sem=s_down.at[d], recv_sem=r_down.at[d],
             device_id={"tp": to}, device_id_type=MESH)
 
-    def codes_start(first, stop):
-        @pl.loop(first, stop)
-        def _(c):
-            for d in range(1, m):
-                code_copy(c, 0, d).start()
-                code_copy(c, 1, d).start()
+    def codes_start(c):
+        for d in range(1, m):
+            code_copy(c, 0, d).start()
+            code_copy(c, 1, d).start()
 
     def normalise(b):
         for d in range(1, m):
@@ -158,8 +203,7 @@
         place = lax.broadcasted_iota(jnp.int32, (rp, n * ns), 0) == row_ref[b]
         place = jnp.where(place, 1.0, 0.0).astype(BF16)
         x_ref[my_part(b), :] = jnp.dot(place, grp[b], preferred_element_type=F32).astype(BF16)
-        for d in range(1, m):
-            x_out(b, d).start()
+        relay(b, 0)
 
     pl.semaphore_wait(barrier, m + n - 2)
     for b in range(BLOCKS):
@@ -168,26 +212,24 @@
     if here:
         for d in range(1, m):
             scale_copy(d).start()
-    early = min(2, chunks)
-    codes_start(0, early)
+            scale_down_copy(d).start()
+    codes_start(0)
     for b in range(BLOCKS):
         wide[b, :, my_feat] = sent[t, b]
     for b in range(BLOCKS):
         normalise(b)
     gather(0)
-    codes_start(early, chunks)
     local[5].wait()
     if here:
         for d in range(1, m):
             scale_copy(d).wait_recv()
     for j in range(depth // 128):
         st[j * 128:(j + 1) * 128, :] = sct[:, j * 128:(j + 1) * 128].T
-    for b in range(1, BLOCKS):
-        gather(b)
-    if here:
-        for d in range(1, m):
-            scale_down_copy(d).start()
-            down_copy(d).start()
+    for phase in range(1, len(far_bits) + 1):
+        relay(0, phase)
+    ahead = min(3, chunks)
+    for c in range(1, ahead):
+        codes_start(c)
     local[0].wait()
     local[1].wait()
 
@@ -215,8 +257,7 @@
 
         @pl.when(c == 0)
         def _():
-            for d in range(1, m):
-                x_out(b, d).wait_recv()
+            x_wait(b)
 
         @pl.when(b == 0)
         def _():
@@ -227,66 +268,72 @@
             xs = x_ref[pl.ds(al(b * rows + side * half, 16), half), :]
             own[side, k] = jnp.dot(xs, both, preferred_element_type=F32).astype(BF16)
 
-    def spot(k, side):
+    piece = half // SUB
+
+    def spot(k, side, u):
         b, c = k // chunks, lax.rem(k, chunks)
-        return hid.at[pl.ds(al(b * rows + side * half, 16), half), pl.ds(al(c * cw, 128), cw)]
-
-    def red_copy(k, side):
-        return pltpu.make_async_remote_copy(
-            src_ref=own.at[side, k], dst_ref=got.at[side, k], send_sem=s_red.at[side, k], recv_sem=r_red.at[side, k],
+        return hid.at[pl.ds(al(b * rows + side * half + u * piece, 16), piece), pl.ds(al(c * cw, 128), cw)]
+
+    def red_copy(k, side, u):
+        there = pl.ds(u * piece, piece)
+        return pltpu.make_async_remote_copy(
+            src_ref=own.at[side, k, there, :], dst_ref=got.at[side, k, there, :],
+            send_sem=s_red.at[side, k, u], recv_sem=r_red.at[side, k, u],
             device_id={"fsdp": jnp.clip(f + (1 if side else -1), 0, last)}, device_id_type=MESH)
 
-    def hid_copy(k, side):
-        return pltpu.make_async_remote_copy(
-            src_ref=spot(k, side), dst_ref=spot(k, side), send_sem=s_hid.at[side, k], recv_sem=r_hid.at[side, k],
+    def hid_copy(k, side, u):
+        return pltpu.make_async_remote_copy(
+            src_ref=spot(k, side, u), dst_ref=spot(k, side, u),
+            send_sem=s_hid.at[side, k, u], recv_sem=r_hid.at[side, k, u],
             device_id={"fsdp": jnp.clip(f + (-1 if side else 1), 0, last)}, device_id_type=MESH)
 
     def valid(k):
         return (k >= 0) & (k < total)
 
-    def reduce_step(s, side):
+    def reduce_step(s, side, u):
         far = f if side else last - f
         k = s - far
+        there = pl.ds(u * piece, piece)
 
         @pl.when(valid(k) & (far > 0))
         def _():
-            red_copy(k, side).wait_recv()
+            red_copy(k, side, u).wait_recv()
 
             @pl.when(far < last)
             def _():
-                own[side, k] = (own[side, k].astype(F32) + got[side, k].astype(F32)).astype(BF16)
+                own[side, k, there] = (own[side, k, there].astype(F32) + got[side, k, there].astype(F32)).astype(BF16)
 
             @pl.when(far == last)
             def _():
-                both = own[side, k].astype(F32) + got[side, k].astype(F32)
+                both = own[side, k, there].astype(F32) + got[side, k, there].astype(F32)
                 gate, up = both[:, :cw], both[:, cw:]
                 b, c = k // chunks, lax.rem(k, chunks)
-                hid[pl.ds(al(b * rows + side * half, 16), half), pl.ds(al(c * cw, 128), cw)] = (
+                hid[pl.ds(al(b * rows + side * half + u * piece, 16), piece), pl.ds(al(c * cw, 128), cw)] = (
                     jax.nn.silu(gate) * up).astype(BF16)
 
-    def reduce_send(s, side):
+    def reduce_send(s, side, u):
         far = f if side else last - f
         k = s - far
 
         @pl.when(valid(k) & (far < last))
         def _():
-            red_copy(k, side).start()
+            red_copy(k, side, u).start()
 
         @pl.when(valid(k) & (far == last))
         def _():
-            hid_copy(k, side).start()
-
-    def pass_on(s, side):
+            hid_copy(k, side, u).start()
+
+    def pass_on(s, side, u):
         far = f if side else last - f
         k = s - last - (last - far)
 
         @pl.when(valid(k) & (far < last))
         def _():
-            hid_copy(k, side).wait_recv()
+            hid_copy(k, side, u).wait_recv()
 
             @pl.when(far > 0)
             def _():
-                hid_copy(k, side).start()
+                hid_copy(k, side, u).start()
 
     def down_weights():
         for i in range(2, 5):
@@ -341,6 +388,13 @@
 
     steps = total + 2 * last
     tasks = [(chunks - 1 + 2 * last, down_weights)]
+    for b in range(1, BLOCKS):
+        tasks.append((1, functools.partial(gather, b)))
+        for phase in range(1, len(far_bits) + 1):
+            tasks.append((1 + 2 * phase, functools.partial(relay, b, phase)))
+    if here:
+        for d in range(1, m):
+            tasks.append((max(chunks - ahead, 0) + d, down_copy(d).start))
     for b in range(BLOCKS):
         at = (b + 1) * chunks - 1 + 2 * last
         tasks += [(at, functools.partial(down, b)), (at + 4, functools.partial(send_back, b)),
@@ -350,12 +404,18 @@
 
     @pl.loop(0, steps)
     def _(s):
-        for side in range(2):
-            reduce_step(s, side)
-        for side in range(2):
-            reduce_send(s, side)
-        for side in range(2):
-            pass_on(s, side)
+        for u in range(SUB):
+            for side in range(2):
+                reduce_step(s, side, u)
+            for side in range(2):
+                reduce_send(s, side, u)
+        for u in range(SUB):
+            for side in range(2):
+                pass_on(s, side, u)
+
+        @pl.when(s + ahead < chunks)
+        def _():
+            codes_start(s + ahead)
 
         @pl.when(s + 1 < total)
         def _():
@@ -383,8 +443,9 @@
             scale_down_copy(d).wait_send()
     for b in range(BLOCKS):
         for d in range(1, m):
-            for out in (rows_out, x_out, sum_out, home_out):
+            for out in (rows_out, sum_out, home_out):
                 out(b, d).wait_send()
+        x_sent(b)
         for d in range(1, n):
             for out in (normed_out, back_out):
                 out(b, d).wait_send()
@@ -396,11 +457,13 @@
 
             @pl.when(far < last)
             def _():
-                red_copy(k, side).wait_send()
+                for u in range(SUB):
+                    red_copy(k, side, u).wait_send()
 
             @pl.when(far > 0)
             def _():
-                hid_copy(k, side).wait_send()
+                for u in range(SUB):
+                    hid_copy(k, side, u).wait_send()
 
 
 def layer(n, m, here, sent, gain, row_of, col_of, code_gate, code_up, scales, base_gate, base_up,
@@ -431,7 +494,8 @@
             vm((BLOCKS, n, ns, depth), BF16), vm((BLOCKS, ns, width), BF16),
             vm((depth, 128), F32), vm((128, depth), F32), vm((chunks, depth), F32),
             dma((chunks, 2, m)), dma((chunks, 2, m)), dma((m,)), dma((m,)), dma((6,)), dma((2, 2)),
-            dma((2, total)), dma((2, total)), dma((2, total)), dma((2, total)),
+            dma((2, total, SUB)), dma((2, total, SUB)), dma((2, total, SUB)), dma((2, total, SUB)),
+            dma((BLOCKS, 2, m)), dma((BLOCKS, 2, m)),
             dma((4, BLOCKS, m)), dma((4, BLOCKS, m)), dma((2, BLOCKS, n)), dma((2, BLOCKS, n)), dma((2, m)), dma((2, m)),
         ],
         compiler_params=pltpu.CompilerParams(

time: 295 us -> 287 us (0.973)
  Pallas kernels: 266 us -> 258 us
    pallas_call x1, Pallas kernels: 266 us -> 258 us  [layer(): pl.pallas_call(functools.partial(layer_kernel, n, m, here), out_shape=jax...]
where the time goes in v3:
time: 287 us; the launch traced here: 285 us
  Pallas kernels  258 us (90%)
  blocking collectives  12.9 us (4%)
  matrix products  6.28 us (2%)
  other arithmetic  4.31 us (2%)
    pallas_call x1, Pallas kernels, layer(): pl.pallas_call(functools.partial(layer_kernel, n, m, here), out_shape=jax...  258 us
    all_gather x1, blocking collectives, shards(): bounds_all = lax.all_gather(cu_seqlens, 'fsdp', axis=0, tiled=True)  12.9 us

profile of v3, /device:TPU:0, one launch (start us, length us, event | category | flops | bytes accessed | tf_op | source)
XLA Modules:
  0.0 285.1 jit_solution(17364322277532080426)
XLA Ops:
  0.6 0.0 copy-start
  0.6 0.0 copy-start.1
  0.7 12.9 %all-gather = s32[4,1,9]{2,1,0:T(1,128)S(1)} all-gather(s32[1,1,9]{2,1,0:T(1,128)} %bitcast.28), channel_id=1, replica_groups=mesh['fsdp'=4,'tp'=8] {'fsdp'}, dimensions={0}, use_global_device_ids=true | all-gather | bytes 180 | tf_op jit(solution)/shard_map/all_gather | solution.py:518
  13.6 0.2 slice_reduce_fusion
  13.8 0.1 reduce
  13.9 0.6 dynamic_slice.7
  14.5 0.7 add_select_fusion.1
  15.2 0.1 broadcast_add_fusion
  15.3 0.1 add.170
  15.4 0.5 constant_dynamic-slice_fusion
  15.9 0.6 compare_select_fusion
  16.4 0.0 copy-start.4
  16.4 0.0 copy-start.2
  16.4 2.9 %fusion.2 = bf16[768,512]{1,0:T(8,128)(2,1)} fusion(bf16[752,512]{1,0:T(8,128)(2,1)} %param.12, s32[768]{0:T(1024)S(1)} %compare_select_fusion), kind=kOutput, calls=%fused_computation.4 | convolution fusion | flops 592367616 | bytes 1559552 | tf_op jit(solution)/shard_map/dot_general | solution.py:528
  19.3 0.1 and_select_fusion.1
  19.4 0.0 copy-done.4
  19.4 0.1 add.174
  19.5 0.1 add.190
  19.6 0.1 add.180
  19.7 0.1 add.181
  19.7 0.1 lt.86
  19.8 0.1 lt.87
  19.9 0.1 add.177
  20.0 0.9 fusion.7.refs_3_
  20.9 0.1 add.175
  21.0 0.6 compare_select_fusion.1.refs_2_
  21.6 0.0 copy-done
  21.6 0.0 copy-done.1
  21.6 0.6 maximum_bitcast_fusion.refs_6_
  22.2 0.0 copy-done.2
  22.3 0.6 reshape.441.refs_10_
  22.9 258.1 %shard_map.131 = bf16[8,2,48,512]{3,2,1,0:T(8,128)(2,1)} custom-call(bf16[8,2,48,512]{3,2,1,0:T(8,128)(2,1)} %bitcast.24, f32[1,4096]{1,0:T(1,128)} %bitcast.26, s32[2,1,192]{2,1,0:T(1,128)} %compare_select_fusion.1.refs_2_, s32[2,192,1]{2,1,0:T(8,128)} %fusion.7.refs_3_, bf16[128,12288]{1,0:T(8,128)(2,1)} %refs_4_.1, bf16[128,12288]{1,0:T(8,128)(2,1)} %refs_5_.1, ...), custom_call_target="tpu_custom_call" | custom-call | tf_op jit(solution)/shard_map/pallas_call | solution.py:483
  281.0 0.0 copy-start.3
  281.0 0.6 iota_compare_fusion.12
  281.5 2.6 fusion.3
  284.1 0.0 copy-done.3
  284.1 0.0 copy-start.5
  284.1 0.1 slice_bitcast_fusion.1
  284.2 0.1 subtract_convert_fusion
  284.3 0.9 convolution_divide_fusion
  285.1 0.0 copy-done.5
  (8 shorter events, 0.1 us)
Async XLA Ops:
  0.6 20.9 %copy-start = (f32[128,96]{0,1:T(8,128)S(1)}, f32[128,96]{0,1:T(8,128)}, u32[]{:S(2)}) copy-start(f32[128,96]{0,1:T(8,128)} %param.19) | copy-start | bytes 147460
  0.6 20.9 %copy-start.1 = (f32[128,96]{0,1:T(8,128)S(1)}, f32[128,96]{0,1:T(8,128)}, u32[]{:S(2)}) copy-start(f32[128,96]{0,1:T(8,128)} %param.20) | copy-start | bytes 147460
  16.4 3.0 %copy-start.4 = (s32[768]{0:T(1024)}, s32[768]{0:T(1024)S(1)}, u32[]{:S(2)}) copy-start(s32[768]{0:T(1024)S(1)} %compare_select_fusion) | copy-start | bytes 9220
  16.4 5.8 %copy-start.2 = (f32[96,128]{1,0:T(8,128)S(1)}, f32[96,128]{1,0:T(8,128)}, u32[]{:S(2)}) copy-start(f32[96,128]{1,0:T(8,128)} %param.22) | copy-start | bytes 147460
  281.0 3.1 %copy-start.3 = (s32[1,9]{1,0:T(1,128)S(1)}, s32[1,9]{1,0:T(1,128)}, u32[]{:S(2)}) copy-start(s32[1,9]{1,0:T(1,128)} %param.23) | copy-start | bytes 112
  284.1 1.0 copy-start.5

commit v4 on v3

--- a/solution.py
+++ b/solution.py
@@ -10,6 +10,7 @@
 EPSILON = 1e-06
 BLOCKS = 2
 SUB = 2
+QUARTERS = 4
 F32, BF16 = jnp.float32, jnp.bfloat16
 MESH = pl.DeviceIdType.MESH
 
@@ -19,10 +20,11 @@
 
 
 def layer_kernel(n, m, here, *refs):
-    (sent, gain_ref, row_ref, col_ref, cg_in, cu_in, sg_in, bg_in, bu_in, cd_in, sd_in, bd_in, out_ref,
+    (tok_ref, gain_ref, cu_ref, cg_in, cu_in, sg_in, bg_in, bu_in, cd_in, sd_in, bd_in, out_ref,
      cg, cu, base, own, got, hid, cd, bd, x_ref, wide, cut, grp, part_out, part_in, back, back_wide, st, sct, sd,
+     sent, home, bounds,
      s_code, r_code, s_down, r_down, l_sem, b_sem, s_red, r_red, s_hid, r_hid, s_x, r_x,
-     s_tp, r_tp, s_fs, r_fs, s_sc, r_sc) = refs
+     s_tp, r_tp, s_fs, r_fs, s_sc, r_sc, s_sum, r_sum, s_back, r_back, s_bound, r_bound) = refs
     f, t = lax.axis_index("fsdp"), lax.axis_index("tp")
     kr = cg_in.shape[0]
     depth, units = cg.shape
@@ -31,7 +33,12 @@
     rows = x_ref.shape[0] // BLOCKS
     half = rows // 2
     rp = rows // m
-    ns, feat = sent.shape[2], sent.shape[3]
+    cap, feat = tok_ref.shape
+    ns = wide.shape[1]
+    lanes = BLOCKS * m
+    lane_bits, part_bits = lanes.bit_length() - 1, m.bit_length() - 1
+    dq = depth // QUARTERS
+    per = QUARTERS // (m // n)
     nb2 = sg_in.shape[-2]
     total = BLOCKS * chunks
     last = n - 1
@@ -87,8 +94,11 @@
     def my_part(b):
         return pl.ds(al(b * rows + t * rp, 16), rp)
 
+    def home_rows(part, b):
+        return pl.ds(al((part * BLOCKS + b) * ns, 16), ns)
+
     def rows_out(b, d):
-        return to_tp(b, 0, d, sent.at[lax.rem(t + d, m), b], wide.at[b, :, my_feat])
+        return to_tp(b, 0, d, sent.at[home_rows(lax.rem(t + d, m), b), :], wide.at[b, :, my_feat])
 
     def normed_out(b, d):
         return to_fs(b, 0, d, cut.at[b, lax.rem(f + d, n)], grp.at[b, pl.ds(al(f * ns, 16), ns), :])
@@ -142,14 +152,55 @@
                 for bit in onward(h, mask) + [1]:
                     x_copy(b, h, mask, bit).wait_send()
 
-    def sum_out(b, d):
-        return to_tp(b, 2, d, part_out.at[b, lax.rem(t + d, m)], part_in.at[b, t])
-
-    def back_out(b, d):
-        return to_fs(b, 1, d, back.at[b, lax.rem(f + d, n)], back_wide.at[b, :, my_depth])
+    def sum_out(b, q, d):
+        return pltpu.make_async_remote_copy(
+            src_ref=part_out.at[b, q, pl.ds(al(lax.rem(t + d, m) * rp, 16), rp), :], dst_ref=part_in.at[b, q, t],
+            send_sem=s_sum.at[b, q, d], recv_sem=r_sum.at[b, q, d],
+            device_id={"tp": lax.rem(t + d, m)}, device_id_type=MESH)
+
+    def quarter(q):
+        return pl.ds(al(f * depth + q * dq, 128), dq)
+
+    def back_out(b, q, d):
+        return pltpu.make_async_remote_copy(
+            src_ref=back.at[b, q, lax.rem(f + d, n)], dst_ref=back_wide.at[b, :, quarter(q)],
+            send_sem=s_back.at[b, q, d], recv_sem=r_back.at[b, q, d],
+            device_id={"fsdp": lax.rem(f + d, n)}, device_id_type=MESH)
 
     def home_out(b, d):
-        return to_tp(b, 3, d, back_wide.at[b, :, pl.ds(al(lax.rem(t + d, m) * feat, 128), feat)], out_ref.at[t, b])
+        return to_tp(b, 1, d, back_wide.at[b, :, pl.ds(al(lax.rem(t + d, m) * feat, 128), feat)],
+                     home.at[home_rows(t, b), :])
+
+    def bound_copy(d):
+        return pltpu.make_async_remote_copy(
+            src_ref=cu_ref, dst_ref=bounds.at[f], send_sem=s_bound.at[d], recv_sem=r_bound.at[d],
+            device_id={"fsdp": lax.rem(f + d, n)}, device_id_type=MESH)
+
+    def group_counts():
+        counts = [bounds[g][:, SEQS:SEQS + 1] for g in range(n)]
+        starts = [jnp.zeros_like(counts[0])]
+        for g in range(1, n):
+            starts.append(starts[-1] + counts[g - 1])
+        return starts, counts
+
+    def home_index(axis):
+        starts, counts = group_counts()
+        start = sum(jnp.where(f == g, starts[g], 0) for g in range(n))
+        live = sum(jnp.where(f == g, counts[g], 0) for g in range(n))
+        shape = (cap, 1) if axis == 0 else (1, cap)
+        r = lax.broadcasted_iota(jnp.int32, shape, axis)
+        lane = (r + start) & (lanes - 1)
+        index = ((lane & (m - 1)) * BLOCKS + (lane >> part_bits)) * ns + (r >> lane_bits)
+        return jnp.where(r < live, index, -1)
+
+    def slot_index(b, g, axis):
+        starts, counts = group_counts()
+        shape = (ns, 1) if axis == 0 else (1, ns)
+        r = ((t + m * b - starts[g]) & (lanes - 1)) + lanes * lax.broadcasted_iota(jnp.int32, shape, axis)
+        return jnp.where(r < counts[g], (starts[g] + r) >> lane_bits, -1)
+
+    def ones_at(mask):
+        return jnp.where(mask, 1.0, 0.0).astype(BF16)
 
     def scale_copy(d):
         to = lax.rem(t + d, m)
@@ -200,12 +251,25 @@
     def gather(b):
         for d in range(1, n):
             normed_out(b, d).wait_recv()
-        place = lax.broadcasted_iota(jnp.int32, (rp, n * ns), 0) == row_ref[b]
-        place = jnp.where(place, 1.0, 0.0).astype(BF16)
-        x_ref[my_part(b), :] = jnp.dot(place, grp[b], preferred_element_type=F32).astype(BF16)
+        mine_x = jnp.zeros((rp, depth), F32)
+        for g in range(n):
+            place = ones_at(lax.broadcasted_iota(jnp.int32, (rp, ns), 0) == slot_index(b, g, 1))
+            mine_x = mine_x + jnp.dot(place, grp[b, g * ns:(g + 1) * ns, :], preferred_element_type=F32)
+        x_ref[my_part(b), :] = mine_x.astype(BF16)
         relay(b, 0)
 
     pl.semaphore_wait(barrier, m + n - 2)
+    for d in range(1, n):
+        bound_copy(d).start()
+    codes_start(0)
+    bounds[f] = cu_ref[...]
+    for d in range(1, n):
+        bound_copy(d).wait_recv()
+    place_of = home_index(1)
+    step = 2 * BLOCKS * ns
+    for i in range(m // 2):
+        spread = ones_at(lax.broadcasted_iota(jnp.int32, (step, cap), 0) + i * step == place_of)
+        sent[i * step:(i + 1) * step, :] = jnp.dot(spread, tok_ref[...], preferred_element_type=F32).astype(BF16)
     for b in range(BLOCKS):
         for d in range(1, m):
             rows_out(b, d).start()
@@ -213,9 +277,8 @@
         for d in range(1, m):
             scale_copy(d).start()
             scale_down_copy(d).start()
-    codes_start(0)
     for b in range(BLOCKS):
-        wide[b, :, my_feat] = sent[t, b]
+        wide[b, :, my_feat] = sent[home_rows(t, b), :]
     for b in range(BLOCKS):
         normalise(b)
     gather(0)
@@ -349,42 +412,39 @@
             cd[there, :] = (bd[there, :].astype(F32) + cd[there, :].astype(F32) * sd[pl.ds(c, 1), :]).astype(BF16)
 
     def down(b):
-        for j in reversed(range(m // 2)):
-            first = lax.rem(t // 2 + j, m // 2) * 2
-            both = jnp.dot(hid[pl.ds(al(b * rows + first * rp, 16), 2 * rp), :], cd[...], preferred_element_type=F32)
-            both = both.astype(BF16)
-            part_out[b, first] = both[:rp]
-            part_out[b, first + 1] = both[rp:]
-            for e in range(2):
-                d = lax.rem(first + e - t + m, m)
-                if j:
-                    sum_out(b, d).start()
-                else:
-                    @pl.when(d > 0)
-                    def _():
-                        sum_out(b, d).start()
-
-    def send_back(b):
-        acc = part_out[b, t].astype(F32)
-        for d in range(1, m):
-            sum_out(b, d).wait_recv()
-        for d in range(1, m):
-            acc = acc + part_in[b, lax.rem(t + d, m)].astype(F32)
-        place = lax.broadcasted_iota(jnp.int32, (n * ns, rp), 1) == col_ref[b]
-        place = jnp.where(place, 1.0, 0.0).astype(BF16)
-        spread = jnp.dot(place, acc.astype(BF16), preferred_element_type=F32).astype(BF16)
+        for q in range(QUARTERS):
+            block = jnp.dot(hid[pl.ds(al(b * rows, 16), rows), :], cd[:, q * dq:(q + 1) * dq],
+                            preferred_element_type=F32)
+            part_out[b, q] = block.astype(BF16)
+            for d in range(1, m):
+                sum_out(b, q, d).start()
+
+    def send_back(b, q):
+        acc = part_out[b, q, pl.ds(al(t * rp, 16), rp), :].astype(F32)
+        for d in range(1, m):
+            sum_out(b, q, d).wait_recv()
+        for d in range(1, m):
+            acc = acc + part_in[b, q, lax.rem(t + d, m)].astype(F32)
+        acc = acc.astype(BF16)
         for g in range(n):
-            back[b, g] = spread[g * ns:(g + 1) * ns]
+            place = ones_at(lax.broadcasted_iota(jnp.int32, (ns, rp), 1) == slot_index(b, g, 0))
+            back[b, q, g] = jnp.dot(place, acc, preferred_element_type=F32).astype(BF16)
         for d in range(1, n):
-            back_out(b, d).start()
-        back_wide[b, :, my_depth] = back[b, f]
-
-    def send_home(b):
-        for d in range(1, n):
-            back_out(b, d).wait_recv()
-        for d in range(1, m):
-            home_out(b, d).start()
-        out_ref[t, b] = back_wide[b, :, my_feat]
+            back_out(b, q, d).start()
+        back_wide[b, :, quarter(q)] = back[b, q, f]
+
+    def send_home(b, h):
+        for q in range(h * per, (h + 1) * per):
+            for d in range(1, n):
+                back_out(b, q, d).wait_recv()
+        for d in range(1, m):
+            @pl.when(lax.rem(lax.rem(t + d, m), m // n) == h)
+            def _():
+                home_out(b, d).start()
+
+        @pl.when(lax.rem(t, m // n) == h)
+        def _():
+            home[home_rows(t, b), :] = back_wide[b, :, my_feat]
 
     steps = total + 2 * last
     tasks = [(chunks - 1 + 2 * last, down_weights)]
@@ -394,11 +454,14 @@
             tasks.append((1 + 2 * phase, functools.partial(relay, b, phase)))
     if here:
         for d in range(1, m):
-            tasks.append((max(chunks - ahead, 0) + d, down_copy(d).start))
+            tasks.append((max(chunks - 3, 0) + d, down_copy(d).start))
     for b in range(BLOCKS):
         at = (b + 1) * chunks - 1 + 2 * last
-        tasks += [(at, functools.partial(down, b)), (at + 4, functools.partial(send_back, b)),
-                  (at + 6, functools.partial(send_home, b))]
+        tasks.append((at, functools.partial(down, b)))
+        for q in range(QUARTERS):
+            tasks.append((at + 3 + q // 2, functools.partial(send_back, b, q)))
+            if q % per == per - 1:
+                tasks.append((at + 5 + q // 2, functools.partial(send_home, b, q // per)))
 
     partial(0)
 
@@ -424,12 +487,17 @@
             if at < steps:
                 pl.when(s == at)(task)
 
-    for at, task in tasks:
-        if at >= steps:
-            task()
+    late = [task for at, task in tasks if at >= steps]
+    for task in late:
+        task()
     for b in range(BLOCKS):
         for d in range(1, m):
             home_out(b, d).wait_recv()
+    place_of = home_index(0)
+    for i in range(0, cap, 256):
+        stop = min(i + 256, cap)
+        spread = ones_at(lax.broadcasted_iota(jnp.int32, (stop - i, m * BLOCKS * ns), 1) == place_of[i:stop])
+        out_ref[i:stop, :] = jnp.dot(spread, home[...], preferred_element_type=F32).astype(BF16)
 
     @pl.loop(0, chunks)
     def _(c):
@@ -443,12 +511,18 @@
             scale_down_copy(d).wait_send()
     for b in range(BLOCKS):
         for d in range(1, m):
-            for out in (rows_out, sum_out, home_out):
+            for out in (rows_out, home_out):
                 out(b, d).wait_send()
+            for q in range(QUARTERS):
+                sum_out(b, q, d).wait_send()
         x_sent(b)
         for d in range(1, n):
-            for out in (normed_out, back_out):
-                out(b, d).wait_send()
+            normed_out(b, d).wait_send()
+            for q in range(QUARTERS):
+                back_out(b, q, d).wait_send()
+
+    for d in range(1, n):
+        bound_copy(d).wait_send()
 
     @pl.loop(0, total)
     def _(k):
@@ -466,72 +540,55 @@
                     hid_copy(k, side, u).wait_send()
 
 
-def layer(n, m, here, sent, gain, row_of, col_of, code_gate, code_up, scales, base_gate, base_up,
-          code_down, scale_down, base_down, live_all):
+def layer(n, m, here, tokens, gain, cu_seqlens, code_gate, code_up, scales, base_gate, base_up,
+          code_down, scale_down, base_down):
     width, units = base_gate.shape
     depth = width // n
-    ns, feat = sent.shape[2:]
+    cap, feat = tokens.shape
+    live_all = n * (cap // 2 + SEQS)
+    ns = -(-(-(-cap // (BLOCKS * m))) // 16) * 16
     chunks = scale_down.shape[-2]
     cw = units // chunks
     total = BLOCKS * chunks
     half = live_all // (2 * BLOCKS)
     rp = live_all // (BLOCKS * m)
+    dq = depth // QUARTERS
     anywhere = pl.BlockSpec(memory_space=pl.ANY)
     near = pl.BlockSpec(memory_space=pltpu.VMEM)
     dma = pltpu.SemaphoreType.DMA
     vm = pltpu.VMEM
     return pl.pallas_call(
         functools.partial(layer_kernel, n, m, here),
-        out_shape=jax.ShapeDtypeStruct((m, BLOCKS, ns, feat), BF16),
-        in_specs=[near, near, near, near] + [anywhere] * 8,
+        out_shape=jax.ShapeDtypeStruct((cap, feat), BF16),
+        in_specs=[near, near, near] + [anywhere] * 8,
         out_specs=near,
         scratch_shapes=[
             vm((depth, units), BF16), vm((depth, units), BF16), vm((2, 2, depth, cw), BF16),
             vm((2, total, half, 2 * cw), BF16), vm((2, total, half, 2 * cw), BF16),
             vm((live_all, units), BF16), vm((units, depth), BF16), vm((units, depth), BF16),
             vm((live_all, depth), BF16), vm((BLOCKS, ns, width), BF16), vm((BLOCKS, n, ns, depth), BF16),
-            vm((BLOCKS, n * ns, depth), BF16), vm((BLOCKS, m, rp, depth), BF16), vm((BLOCKS, m, rp, depth), BF16),
-            vm((BLOCKS, n, ns, depth), BF16), vm((BLOCKS, ns, width), BF16),
+            vm((BLOCKS, n * ns, depth), BF16), vm((BLOCKS, QUARTERS, m * rp, dq), BF16),
+            vm((BLOCKS, QUARTERS, m, rp, dq), BF16), vm((BLOCKS, QUARTERS, n, ns, dq), BF16),
+            vm((BLOCKS, ns, width), BF16),
             vm((depth, 128), F32), vm((128, depth), F32), vm((chunks, depth), F32),
+            vm((m * BLOCKS * ns, feat), BF16), vm((m * BLOCKS * ns, feat), BF16), vm((n,) + cu_seqlens.shape, jnp.int32),
             dma((chunks, 2, m)), dma((chunks, 2, m)), dma((m,)), dma((m,)), dma((6,)), dma((2, 2)),
             dma((2, total, SUB)), dma((2, total, SUB)), dma((2, total, SUB)), dma((2, total, SUB)),
             dma((BLOCKS, 2, m)), dma((BLOCKS, 2, m)),
-            dma((4, BLOCKS, m)), dma((4, BLOCKS, m)), dma((2, BLOCKS, n)), dma((2, BLOCKS, n)), dma((2, m)), dma((2, m)),
+            dma((2, BLOCKS, m)), dma((2, BLOCKS, m)), dma((1, BLOCKS, n)), dma((1, BLOCKS, n)), dma((2, m)), dma((2, m)),
+            dma((BLOCKS, QUARTERS, m)), dma((BLOCKS, QUARTERS, m)), dma((BLOCKS, QUARTERS, n)), dma((BLOCKS, QUARTERS, n)),
+            dma((n,)), dma((n,)),
         ],
         compiler_params=pltpu.CompilerParams(
             collective_id=0, has_side_effects=True, vmem_limit_bytes=67043328),
-    )(sent, gain, row_of, col_of, code_gate, code_up, scales, base_gate, base_up, code_down, scale_down, base_down)
+    )(tokens, gain, cu_seqlens, code_gate, code_up, scales, base_gate, base_up, code_down, scale_down, base_down)
 
 
 def shards(tokens, norm_gain, base_gate, base_up, base_down, code_gate, code_up,
            scale_gate, scale_up, code_down, scale_down, cu_seqlens):
     n, m = lax.axis_size("fsdp"), lax.axis_size("tp")
-    me_f, me_t = lax.axis_index("fsdp"), lax.axis_index("tp")
-    cap, feat = tokens.shape
-    live_all = n * (cap // 2 + SEQS)
-    lanes = BLOCKS * m
-    rp = live_all // lanes
-    ns = -(-(-(-cap // lanes)) // 16) * 16
     kr = code_gate.shape[0]
     nb = scale_gate.shape[1] // m
-
-    bounds_all = lax.all_gather(cu_seqlens, "fsdp", axis=0, tiled=True)
-    counts = bounds_all[:, SEQS]
-    starts = jnp.cumsum(counts) - counts
-    start, live = starts[me_f], counts[me_f]
-
-    q_of = (jnp.arange(m)[:, None] + m * jnp.arange(BLOCKS)[None, :])
-    row_of = ((q_of - start) % lanes)[:, :, None] + lanes * jnp.arange(ns)[None, None, :]
-    row_of = jnp.where(row_of < live, row_of, -1).reshape(-1)
-    slots = jnp.arange(cap, dtype=jnp.int32)
-    spread = (row_of[:, None] == slots[None, :]).astype(BF16)
-    sent = jnp.dot(spread, tokens, preferred_element_type=F32).astype(BF16)
-
-    q_mine = me_t + m * jnp.arange(BLOCKS)
-    r_all = ((q_mine[:, None] - starts[None, :]) % lanes)[:, :, None] + lanes * jnp.arange(ns)[None, None, :]
-    slot_all = jnp.where(r_all < counts[None, :, None], (starts[None, :, None] + r_all) // lanes, -1)
-    slot_all = slot_all.reshape(BLOCKS, n * ns)
-
     scales = jnp.concatenate([scale_gate.reshape(kr, m, nb), scale_up.reshape(kr, m, nb)], axis=2).transpose(1, 2, 0)
     scales = jnp.pad(scales, ((0, 0), (0, -(2 * nb) % 8), (0, 0)))
     scale_down = scale_down.reshape(m, nb, -1)
@@ -540,15 +597,13 @@
         code_down = lax.all_to_all(code_down, "tp", split_axis=0, concat_axis=1, tiled=True)
         scales = lax.all_to_all(scales, "tp", split_axis=0, concat_axis=2, tiled=True)[0]
         scale_down = lax.all_to_all(scale_down, "tp", split_axis=0, concat_axis=2, tiled=True)[0]
-    home = layer(n, m, here, sent.reshape(m, BLOCKS, ns, feat), norm_gain[None, :], slot_all[:, None, :],
-                 slot_all[:, :, None], code_gate, code_up, scales, base_gate, base_up, code_down, scale_down,
-                 base_down, live_all)
-    summed_out = lax.dot_general(spread, home.reshape(m * BLOCKS * ns, feat), (((0,), (0,)), ((), ())),
-                                 preferred_element_type=F32)
+    summed_out = layer(n, m, here, tokens, norm_gain[None, :], cu_seqlens, code_gate, code_up, scales,
+                       base_gate, base_up, code_down, scale_down, base_down)
 
     bounds = cu_seqlens[0]
-    mixed = (tokens.astype(F32) + summed_out).astype(BF16)
-    mixed = jnp.where((slots < live)[:, None], mixed, jnp.zeros((), BF16))
+    slots = jnp.arange(tokens.shape[0], dtype=jnp.int32)
+    mixed = (tokens.astype(F32) + summed_out.astype(F32)).astype(BF16)
+    mixed = jnp.where((slots < bounds[SEQS])[:, None], mixed, jnp.zeros((), BF16))
     member = (slots[None, :] >= bounds[:-1, None]) & (slots[None, :] < bounds[1:, None])
     seq_sums = jnp.dot(member.astype(BF16), mixed, preferred_element_type=F32)
     lengths = (bounds[1:] - bounds[:-1]).astype(F32)

time: 287 us -> 283 us (0.986)
  blocking collectives: 12.9 us -> 0 us
  Pallas kernels: 258 us -> 270 us
  matrix products: 6.28 us -> 0.86 us
    all_gather x1 -> x0, blocking collectives: 12.9 us -> none  [shards(): bounds_all = lax.all_gather(cu_seqlens, 'fsdp', axis=0, tiled=True)]
    pallas_call x1, Pallas kernels: 258 us -> 270 us  [layer(): pl.pallas_call(functools.partial(layer_kernel, n, m, here), out_shape=jax...]
    dot_general x2 -> x0, matrix products: 5.42 us -> none  [the longest x1 2.86 us: shards(): sent = jnp.dot(spread, tokens, preferred_element_type=F32).astype(BF16)]
where the time goes in v4:
time: 283 us; the launch traced here: 280 us
  Pallas kernels  270 us (95%)
  local copies, waits for them, and re-layouts  5.1 us (2%)
  other arithmetic  3.72 us (1%)
    pallas_call x1, Pallas kernels, layer(): pl.pallas_call(functools.partial(layer_kernel, n, m, here), out_shape=jax...  270 us

profile of v4, /device:TPU:0, one launch (start us, length us, event | category | flops | bytes accessed | tf_op | source)
XLA Modules:
  0.0 280.0 jit_solution(5111981827189558)
XLA Ops:
  0.6 0.8 reshape.35
  1.4 0.8 reshape.36
  2.2 0.7 maximum_bitcast_fusion.refs_5_
  2.9 1.4 reshape.37.refs_9_
  4.3 269.7 %shard_map.131 = bf16[752,512]{1,0:T(8,128)(2,1)} custom-call(bf16[752,512]{1,0:T(8,128)(2,1)} %refs_0_.1, f32[1,4096]{1,0:T(1,128)} %bitcast.17, s32[1,9]{1,0:T(1,128)} %refs_2_.1, bf16[128,12288]{1,0:T(8,128)(2,1)} %refs_3_.1, bf16[128,12288]{1,0:T(8,128)(2,1)} %refs_4_.1, f32[8,24,128]{2,1,0:T(8,128)} %maximum_bitcast_fusion.refs_5_, ...), custom_call_target="tpu_custom_call" | custom-call | tf_op jit(solution)/shard_map/pallas_call | solution.py:560
  274.0 1.2 slice.14
  275.3 0.6 iota_compare_fusion.3
  275.9 1.6 fusion
  277.5 0.0 copy-start
  277.5 0.8 slice_bitcast_fusion.1
  278.4 0.8 subtract_convert_fusion
  279.2 0.9 convolution_divide_fusion
  280.0 0.0 copy-done
Async XLA Ops:
  277.5 2.5 copy-start

commit v5 on v4

--- a/solution.py
+++ b/solution.py
@@ -10,7 +10,7 @@
 EPSILON = 1e-06
 BLOCKS = 2
 SUB = 2
-QUARTERS = 4
+QUARTERS = 2
 F32, BF16 = jnp.float32, jnp.bfloat16
 MESH = pl.DeviceIdType.MESH
 
@@ -20,7 +20,7 @@
 
 
 def layer_kernel(n, m, here, *refs):
-    (tok_ref, gain_ref, cu_ref, cg_in, cu_in, sg_in, bg_in, bu_in, cd_in, sd_in, bd_in, out_ref,
+    (tok_ref, gain_ref, cu_ref, cg_in, cu_in, sg_in, bg_in, bu_in, cd_in, sd_in, bd_in, out_ref, mean_ref,
      cg, cu, base, own, got, hid, cd, bd, x_ref, wide, cut, grp, part_out, part_in, back, back_wide, st, sct, sd,
      sent, home, bounds,
      s_code, r_code, s_down, r_down, l_sem, b_sem, s_red, r_red, s_hid, r_hid, s_x, r_x,
@@ -497,7 +497,15 @@
     for i in range(0, cap, 256):
         stop = min(i + 256, cap)
         spread = ones_at(lax.broadcasted_iota(jnp.int32, (stop - i, m * BLOCKS * ns), 1) == place_of[i:stop])
-        out_ref[i:stop, :] = jnp.dot(spread, home[...], preferred_element_type=F32).astype(BF16)
+        summed = jnp.dot(spread, home[...], preferred_element_type=F32)
+        mixed = (tok_ref[i:stop, :].astype(F32) + summed).astype(BF16).astype(F32)
+        out_ref[i:stop, :] = jnp.where(place_of[i:stop] >= 0, mixed, 0.0).astype(BF16)
+    seq = lax.broadcasted_iota(jnp.int32, (SEQS, 1), 0)
+    low = sum(jnp.where(seq == j, cu_ref[:, j:j + 1], 0) for j in range(SEQS))
+    high = sum(jnp.where(seq == j, cu_ref[:, j + 1:j + 2], 0) for j in range(SEQS))
+    row = lax.broadcasted_iota(jnp.int32, (SEQS, cap), 1)
+    member = ones_at((row >= low) & (row < high))
+    mean_ref[...] = jnp.dot(member, out_ref[...], preferred_element_type=F32) / (high - low).astype(F32)
 
     @pl.loop(0, chunks)
     def _(c):
@@ -559,9 +567,9 @@
     vm = pltpu.VMEM
     return pl.pallas_call(
         functools.partial(layer_kernel, n, m, here),
-        out_shape=jax.ShapeDtypeStruct((cap, feat), BF16),
+        out_shape=(jax.ShapeDtypeStruct((cap, feat), BF16), jax.ShapeDtypeStruct((SEQS, feat), F32)),
         in_specs=[near, near, near] + [anywhere] * 8,
-        out_specs=near,
+        out_specs=(near, near),
         scratch_shapes=[
             vm((depth, units), BF16), vm((depth, units), BF16), vm((2, 2, depth, cw), BF16),
             vm((2, total, half, 2 * cw), BF16), vm((2, total, half, 2 * cw), BF16),
@@ -597,17 +605,8 @@
         code_down = lax.all_to_all(code_down, "tp", split_axis=0, concat_axis=1, tiled=True)
         scales = lax.all_to_all(scales, "tp", split_axis=0, concat_axis=2, tiled=True)[0]
         scale_down = lax.all_to_all(scale_down, "tp", split_axis=0, concat_axis=2, tiled=True)[0]
-    summed_out = layer(n, m, here, tokens, norm_gain[None, :], cu_seqlens, code_gate, code_up, scales,
-                       base_gate, base_up, code_down, scale_down, base_down)
-
-    bounds = cu_seqlens[0]
-    slots = jnp.arange(tokens.shape[0], dtype=jnp.int32)
-    mixed = (tokens.astype(F32) + summed_out.astype(F32)).astype(BF16)
-    mixed = jnp.where((slots < bounds[SEQS])[:, None], mixed, jnp.zeros((), BF16))
-    member = (slots[None, :] >= bounds[:-1, None]) & (slots[None, :] < bounds[1:, None])
-    seq_sums = jnp.dot(member.astype(BF16), mixed, preferred_element_type=F32)
-    lengths = (bounds[1:] - bounds[:-1]).astype(F32)
-    return mixed, seq_sums / lengths[:, None]
+    return layer(n, m, here, tokens, norm_gain[None, :], cu_seqlens, code_gate, code_up, scales,
+                 base_gate, base_up, code_down, scale_down, base_down)
 
 
 def solution(mesh):

time: 283 us -> 277 us (0.979)
  other arithmetic: 3.72 us -> 0.65 us
    unnamed x2, local copies, waits for them, and re-layouts: 0.01 us -> 3.37 us
where the time goes in v5:
time: 277 us; the launch traced here: 276 us
  Pallas kernels  268 us (97%)
  local copies, waits for them, and re-layouts  6.4 us (2%)
    pallas_call x1, Pallas kernels, layer(): pl.pallas_call(functools.partial(layer_kernel, n, m, here), out_shape=(ja...  268 us

profile of v5, /device:TPU:0, one launch (start us, length us, event | category | flops | bytes accessed | tf_op | source)
XLA Modules:
  0.0 275.6 jit_solution(15543610117693079577)
XLA Ops:
  0.6 0.8 reshape.13
  1.4 0.8 reshape.14
  2.2 0.7 maximum_bitcast_fusion.refs_5_
  2.9 1.4 reshape.15.refs_9_
  4.3 267.9 %shard_map.131 = (bf16[752,512]{1,0:T(8,128)(2,1)}, f32[8,512]{1,0:T(8,128)}) custom-call(bf16[752,512]{1,0:T(8,128)(2,1)} %refs_0_.1, f32[1,4096]{1,0:T(1,128)} %bitcast.7, s32[1,9]{1,0:T(1,128)} %refs_2_.1, bf16[128,12288]{1,0:T(8,128)(2,1)} %refs_3_.1, bf16[128,12288]{1,0:T(8,128)(2,1)} %refs_4_.1, f32[8,24,128]{2,1,0:T(8,128)} %maximum_bitcast_fusion.refs_5_, ...), custom_call_target="tpu_custom_call" | custom-call | tf_op jit(solution)/shard_map/pallas_call | solution.py:568
  272.2 2.1 copy.16
  274.3 1.3 copy.17

commit v6 on v5

--- a/solution.py
+++ b/solution.py
@@ -261,7 +261,6 @@
     pl.semaphore_wait(barrier, m + n - 2)
     for d in range(1, n):
         bound_copy(d).start()
-    codes_start(0)
     bounds[f] = cu_ref[...]
     for d in range(1, n):
         bound_copy(d).wait_recv()
@@ -277,10 +276,10 @@
         for d in range(1, m):
             scale_copy(d).start()
             scale_down_copy(d).start()
+    codes_start(0)
     for b in range(BLOCKS):
         wide[b, :, my_feat] = sent[home_rows(t, b), :]
-    for b in range(BLOCKS):
-        normalise(b)
+    normalise(0)
     gather(0)
     local[5].wait()
     if here:
@@ -446,12 +445,49 @@
         def _():
             home[home_rows(t, b), :] = back_wide[b, :, my_feat]
 
+    def drain():
+        @pl.loop(0, chunks)
+        def _(c):
+            for d in range(1, m):
+                code_copy(c, 0, d).wait_send()
+                code_copy(c, 1, d).wait_send()
+        if here:
+            for d in range(1, m):
+                down_copy(d).wait_send()
+                scale_copy(d).wait_send()
+                scale_down_copy(d).wait_send()
+        for b in range(BLOCKS):
+            for d in range(1, m):
+                rows_out(b, d).wait_send()
+            x_sent(b)
+            for d in range(1, n):
+                normed_out(b, d).wait_send()
+
+        for d in range(1, n):
+            bound_copy(d).wait_send()
+
+        @pl.loop(0, total)
+        def _(k):
+            for side in range(2):
+                far = f if side else last - f
+
+                @pl.when(far < last)
+                def _():
+                    for u in range(SUB):
+                        red_copy(k, side, u).wait_send()
+
+                @pl.when(far > 0)
+                def _():
+                    for u in range(SUB):
+                        hid_copy(k, side, u).wait_send()
+
     steps = total + 2 * last
     tasks = [(chunks - 1 + 2 * last, down_weights)]
     for b in range(1, BLOCKS):
-        tasks.append((1, functools.partial(gather, b)))
+        tasks.append((0, functools.partial(normalise, b)))
+        tasks.append((3, functools.partial(gather, b)))
         for phase in range(1, len(far_bits) + 1):
-            tasks.append((1 + 2 * phase, functools.partial(relay, b, phase)))
+            tasks.append((3 + 2 * phase, functools.partial(relay, b, phase)))
     if here:
         for d in range(1, m):
             tasks.append((max(chunks - 3, 0) + d, down_copy(d).start))
@@ -488,7 +524,7 @@
                 pl.when(s == at)(task)
 
     late = [task for at, task in tasks if at >= steps]
-    for task in late:
+    for task in [drain] + late:
         task()
     for b in range(BLOCKS):
         for d in range(1, m):
@@ -507,45 +543,14 @@
     member = ones_at((row >= low) & (row < high))
     mean_ref[...] = jnp.dot(member, out_ref[...], preferred_element_type=F32) / (high - low).astype(F32)
 
-    @pl.loop(0, chunks)
-    def _(c):
-        for d in range(1, m):
-            code_copy(c, 0, d).wait_send()
-            code_copy(c, 1, d).wait_send()
-    if here:
-        for d in range(1, m):
-            down_copy(d).wait_send()
-            scale_copy(d).wait_send()
-            scale_down_copy(d).wait_send()
     for b in range(BLOCKS):
         for d in range(1, m):
-            for out in (rows_out, home_out):
-                out(b, d).wait_send()
+            home_out(b, d).wait_send()
             for q in range(QUARTERS):
                 sum_out(b, q, d).wait_send()
-        x_sent(b)
         for d in range(1, n):
-            normed_out(b, d).wait_send()
             for q in range(QUARTERS):
                 back_out(b, q, d).wait_send()
-
-    for d in range(1, n):
-        bound_copy(d).wait_send()
-
-    @pl.loop(0, total)
-    def _(k):
-        for side in range(2):
-            far = f if side else last - f
-
-            @pl.when(far < last)
-            def _():
-                for u in range(SUB):
-                    red_copy(k, side, u).wait_send()
-
-            @pl.when(far > 0)
-            def _():
-                for u in range(SUB):
-                    hid_copy(k, side, u).wait_send()
 
 
 def layer(n, m, here, tokens, gain, cu_seqlens, code_gate, code_up, scales, base_gate, base_up,

time: 277 us -> 273 us (0.986)
  Pallas kernels: 268 us -> 262 us
    pallas_call x1, Pallas kernels: 268 us -> 262 us  [layer(): pl.pallas_call(functools.partial(layer_kernel, n, m, here), out_shape=(ja...]
where the time goes in v6:
time: 273 us; the launch traced here: 270 us
  Pallas kernels  262 us (96%)
  local copies, waits for them, and re-layouts  6.4 us (2%)
    pallas_call x1, Pallas kernels, layer(): pl.pallas_call(functools.partial(layer_kernel, n, m, here), out_shape=(ja...  262 us

profile of v6, /device:TPU:0, one launch (start us, length us, event | category | flops | bytes accessed | tf_op | source)
XLA Modules:
  0.0 269.8 jit_solution(7233137380742222332)
XLA Ops:
  0.6 0.8 reshape.13
  1.4 0.8 reshape.14
  2.2 0.7 maximum_bitcast_fusion.refs_5_
  2.9 1.4 reshape.15.refs_9_
  4.3 262.1 %shard_map.131 = (bf16[752,512]{1,0:T(8,128)(2,1)}, f32[8,512]{1,0:T(8,128)}) custom-call(bf16[752,512]{1,0:T(8,128)(2,1)} %refs_0_.1, f32[1,4096]{1,0:T(1,128)} %bitcast.7, s32[1,9]{1,0:T(1,128)} %refs_2_.1, bf16[128,12288]{1,0:T(8,128)(2,1)} %refs_3_.1, bf16[128,12288]{1,0:T(8,128)(2,1)} %refs_4_.1, f32[8,24,128]{2,1,0:T(8,128)} %maximum_bitcast_fusion.refs_5_, ...), custom_call_target="tpu_custom_call" | custom-call | tf_op jit(solution)/shard_map/pallas_call | solution.py:573
  266.4 2.1 copy.16
  268.4 1.3 copy.17
